TPU v7x, 32 devices: a whole 2x2x4 slice. The times are simulated.
32 devices in a mesh: ctx: 16 (over z, x, core), head: 2 (over y).
Axes of the slice: x: 2, y: 2, z: 4, core: 2. Of those that a mesh axis runs over, the one named last changes fastest.
Arguments:
- queries: bfloat16 [8192, 16, 128], P('ctx', 'head'), may hold values from -160 to 160, as said below
- keys: bfloat16 [8192, 2, 128], P('ctx', 'head'), may hold values from -4 to 4
- values: bfloat16 [8192, 2, 128], P('ctx', 'head'), may hold values from -6 to 6
- doc_lengths: int32 [32], replicated, may hold values from 1 to 4096, 8192 in all
Outputs:
- attended: bfloat16 [8192, 2048], P(('ctx', 'head'))
Inputs may be any that keep to these rules, and one draw needn't show every extreme that they name: `queries`: queries of several heads for a few tokens may be large multiples of sums of earlier keys of the same key head. `doc_lengths`: the lengths sum to 8192; the largest is exactly 4096.
All inputs are finite; a program needn't handle non-finite values.
Results may differ from a plain program's by a relative error of at most 0.0033.
Values may be sent and summed in bfloat16 or wider, within the bound.
A program may use at most 64 MiB of HBM per device.

v0:
```python
import functools
import math

import jax
import jax.numpy as jnp
from jax import lax
from jax.experimental import pallas as pl
from jax.experimental.pallas import tpu as pltpu
from jax.sharding import PartitionSpec as P

MESH = pl.DeviceIdType.MESH
BIG = 1e30
MOST = 1024


def kernel(n, heads, tile, lens_ref, q_ref, k_ref, v_ref, out_ref,
           kbuf, vbuf, kdoc, qaug, acc, top, norm, stage,
           send_sem, recv_sem, osend_sem, orecv_sem):
    rows, hdim = k_ref.shape
    total_rows = q_ref.shape[0]
    group = total_rows // rows
    me = lax.axis_index("ctx")
    mine = lax.axis_index("head")
    pos = me % 4
    core = pos % 2
    col = pos // 2
    mate = me + 1 - 2 * core
    across = me + 2 - 4 * col
    pos_m = pos + 1 - 2 * core
    pos_x = pos + 2 - 4 * col
    pos_d = pos_x + pos_m - pos
    has1 = me >= 4
    has2 = me >= 8
    feeds = me + 4 < n
    right = col == 1
    leftc = col == 0

    barrier = pltpu.get_barrier_semaphore()
    for peer in (mate, across):
        pl.semaphore_signal(barrier, inc=1, device_id={"ctx": peer}, device_id_type=MESH)

    @pl.when(has1)
    def _():
        pl.semaphore_signal(barrier, inc=1, device_id={"ctx": me - 4}, device_id_type=MESH)

    @pl.when(feeds)
    def _():
        pl.semaphore_signal(barrier, inc=1, device_id={"ctx": me + 4}, device_id_type=MESH)

    for d in range(1, heads):
        pl.semaphore_signal(barrier, inc=1, device_id={"head": (mine + d) % heads}, device_id_type=MESH)
    pl.semaphore_wait(barrier, 1 + heads + has1.astype(jnp.int32) + feeds.astype(jnp.int32))

    def copies(lane, slot, to_slot, target):
        made = []
        for w, buf, own in ((0, kbuf, k_ref), (1, vbuf, v_ref)):
            made.append(pltpu.make_async_remote_copy(
                src_ref=own if slot is None else buf.at[slot],
                dst_ref=buf.at[to_slot],
                send_sem=send_sem.at[lane, w],
                recv_sem=recv_sem.at[to_slot, w],
                device_id={"ctx": target},
                device_id_type=MESH,
            ))
        return made

    moves = {
        "D0": (copies(0, None, 8 + pos, mate), None),
        "X0": (copies(1, None, 8 + pos, across), leftc),
        "Z0": (copies(2, None, 4 + pos, me + 4), feeds),
        "D0x": (copies(3, 8 + pos_x, 8 + pos_x, mate), right),
        "D1": (copies(4, 4 + pos, 4 + pos, mate), has1),
        "X1": (copies(5, 4 + pos, 4 + pos, across), has1),
        "Z1": (copies(6, 4 + pos, pos, me + 4), has1 & feeds),
        "D1x": (copies(7, 4 + pos_x, 4 + pos_x, mate), has1),
        "D2": (copies(8, pos, pos, mate), has2),
        "X2": (copies(9, pos, pos, across), has2 & right),
        "D2x": (copies(10, pos_x, pos_x, mate), has2 & leftc),
    }

    def when(cond, fn):
        if cond is None:
            fn()
        else:
            pl.when(cond)(fn)

    def start(name):
        made, cond = moves[name]

        def go():
            for copy in made:
                copy.start()

        when(cond, go)

    def sent(name):
        made, cond = moves[name]

        def go():
            for copy in made:
                copy.wait_send()

        when(cond, go)

    def landed(slot, cond):
        def go():
            for w, buf in ((0, kbuf), (1, vbuf)):
                pltpu.make_async_copy(buf.at[slot], buf.at[slot], recv_sem.at[slot, w]).wait()

        when(cond, go)

    start("Z0")
    start("X0")
    start("D0")

    lane = lax.broadcasted_iota(jnp.int32, (8, 128), 1)
    firsts = jnp.full((8, 128), 2**30, jnp.int32)
    ends = jnp.full((8, 128), 2**30, jnp.int32)
    run = jnp.int32(0)
    for d in range(lens_ref.shape[0]):
        firsts = jnp.where(lane == d, run, firsts)
        run = run + lens_ref[d]
        ends = jnp.where(lane == d, run, ends)
    first_row, end_row = firsts[0:1], ends[0:1]

    def member(position):
        return (position >= first_row) & (position < end_row)

    base = me * rows

    @pl.loop(0, total_rows // tile)
    def _(t):
        at = pl.ds(pl.multiple_of(t * tile, tile), tile)
        token = (t * tile + lax.broadcasted_iota(jnp.int32, (tile, 128), 0)) // group
        qaug[at, 0:hdim] = q_ref[at, :]
        qaug[at, hdim:] = jnp.where(member(base + token), 1.0, 0.0).astype(jnp.bfloat16)

    @pl.loop(0, 12)
    def _(s):
        kpos = (me - pos - 8 + s) * rows + lax.broadcasted_iota(jnp.int32, (rows, 128), 0)
        kdoc[s] = jnp.where(member(kpos), 0.0, -BIG).astype(jnp.bfloat16)

    @pl.when(me < 8)
    def _():
        @pl.loop(0, 4)
        def _(s):
            kbuf[s] = jnp.zeros((rows, hdim), jnp.bfloat16)
            vbuf[s] = jnp.zeros((rows, hdim), jnp.bfloat16)

    scale = math.log2(math.e) / hdim**0.5

    def spread(x, width):
        return jnp.concatenate([x] * (width // 128), axis=1)

    def score(at, keys, docs):
        return lax.dot_general(
            qaug[at, :], jnp.concatenate([keys, docs], axis=1), (((1,), (1,)), ((), ())),
            preferred_element_type=jnp.float32) * scale

    @pl.loop(0, total_rows // tile)
    def _(t):
        at = pl.ds(pl.multiple_of(t * tile, tile), tile)
        s = score(at, k_ref[...], kdoc[8 + pos])
        token = (t * tile + lax.broadcasted_iota(jnp.int32, (tile, rows), 0)) // group
        s = jnp.where(lax.broadcasted_iota(jnp.int32, (tile, rows), 1) <= token, s, -BIG)
        m = jnp.broadcast_to(jnp.max(s, axis=1, keepdims=True), (tile, 128))
        e = jnp.exp2(s - spread(m, rows))
        top[at, :] = m
        acc[at, 0:128] = jnp.dot(e.astype(jnp.bfloat16), v_ref[...], preferred_element_type=jnp.float32)
        acc[at, 128:] = sum(e[:, k * 128:(k + 1) * 128] for k in range(rows // 128))

    def both(at, a, b):
        sa = score(at, kbuf[a], kdoc[a])
        sb = score(at, kbuf[b], kdoc[b])
        m0 = top[at, :]
        m = jnp.maximum(m0, jnp.max(jnp.maximum(sa, sb), axis=1, keepdims=True))
        wide = spread(m, rows)
        ea = jnp.exp2(sa - wide)
        eb = jnp.exp2(sb - wide)
        pa = ea.astype(jnp.bfloat16)
        pb = eb.astype(jnp.bfloat16)
        top[at, :] = m
        grown = jnp.dot(pa, vbuf[a], preferred_element_type=jnp.float32)
        grown = grown + jnp.dot(pb, vbuf[b], preferred_element_type=jnp.float32)
        factor = jnp.exp2(m0 - m)
        tot = sum(ea[:, k * 128:(k + 1) * 128] + eb[:, k * 128:(k + 1) * 128] for k in range(rows // 128))
        return jnp.concatenate([acc[at, 0:128] * factor + grown, acc[at, 128:] * factor + tot], axis=1)

    def pair(a, b, valid):
        @pl.when(valid)
        def _():
            @pl.loop(0, total_rows // tile)
            def _(t):
                at = pl.ds(pl.multiple_of(t * tile, tile), tile)
                acc[at, :] = both(at, a, b)

    def pick(if_right, if_left):
        return col * if_right + (1 - col) * if_left

    g1 = (4 + pos, 4 + pos_m)
    g2 = (4 + pos_x, 4 + pos_d)
    g3 = (pick(8 + pos_x, pos_x), pick(8 + pos_d, pos_d))
    g4 = (pos, core * (8 + pos_m) + (1 - core) * pos_m)

    landed(4 + pos, has1)
    start("Z1")
    start("X1")
    start("D1")
    landed(8 + pos_x, right)
    start("D0x")
    landed(8 + pos_m, None)
    landed(4 + pos_m, has1)
    landed(8 + pos_d, right)
    pair(pick(g3[0], g1[0]), pick(g3[1], g1[1]), right | has1)

    landed(pos, has2)
    start("X2")
    start("D2")
    landed(4 + pos_x, has1)
    start("D1x")
    landed(4 + pos_d, has1)
    pair(pick(g1[0], g2[0]), pick(g1[1], g2[1]), has1)

    landed(pos_m, has2)
    pair(pick(g2[0], g4[0]), pick(g2[1], g4[1]), (right & has1) | (leftc & (has2 | (core == 1))))

    landed(pos_x, has2 & leftc)
    start("D2x")
    landed(pos_d, has2 & leftc)
    last_a, last_b = pick(g4[0], g3[0]), pick(g4[1], g3[1])
    last_valid = has2 | (right & (core == 1))

    part = rows // heads
    tokens = tile // group
    steps = part // tokens
    columns = pl.ds(pl.multiple_of(mine * (group * hdim), group * hdim), group * hdim)

    def finish(owner, t, own):
        at = pl.ds(pl.multiple_of(owner * (part * group) + t * tile, tile), tile)

        @pl.when(last_valid)
        def _():
            whole = both(at, last_a, last_b)
            norm[...] = whole[:, 0:hdim] / jnp.sum(whole[:, hdim:], axis=1, keepdims=True)

        @pl.when(jnp.logical_not(last_valid))
        def _():
            whole = acc[at, :]
            norm[...] = whole[:, 0:hdim] / jnp.sum(whole[:, hdim:], axis=1, keepdims=True)

        local = pl.ds(pl.multiple_of(t * tokens, tokens), tokens)
        for g in range(group):
            piece = norm[pl.ds(g, tokens, stride=group), :].astype(jnp.bfloat16)
            if own is None:
                where = pl.ds(pl.multiple_of(mine * (group * hdim) + g * hdim, hdim), hdim)
                out_ref[local, where] = piece
            else:
                stage[own, local, g * hdim:(g + 1) * hdim] = piece

    def outgoing(d, t):
        local = pl.ds(pl.multiple_of(t * tokens, tokens), tokens)
        return pltpu.make_async_remote_copy(
            src_ref=stage.at[d - 1, local],
            dst_ref=out_ref.at[local, columns],
            send_sem=osend_sem.at[d - 1, t],
            recv_sem=orecv_sem.at[d - 1, t],
            device_id={"head": (mine + d) % heads},
            device_id_type=MESH,
        )

    for d in range(1, heads):
        @pl.loop(0, steps)
        def _(t):
            finish((mine + d) % heads, t, d - 1)
            outgoing(d, t).start()

    @pl.loop(0, steps)
    def _(t):
        finish(mine, t, None)

    for d in range(1, heads):
        @pl.loop(0, steps)
        def _(t):
            outgoing(d, t).wait_send()
            source = (mine + heads - d) % heads
            local = pl.ds(pl.multiple_of(t * tokens, tokens), tokens)
            cols = pl.ds(pl.multiple_of(source * (group * hdim), group * hdim), group * hdim)
            got = out_ref.at[local, cols]
            pltpu.make_async_copy(got, got, orecv_sem.at[d - 1, t]).wait()

    for name in moves:
        sent(name)


def on_device(mesh, queries, keys, values, doc_lengths):
    rows, group, hdim = queries.shape
    heads = mesh.shape["head"]
    n = mesh.shape["ctx"]
    bf16, f32 = jnp.bfloat16, jnp.float32
    part = rows // heads
    tile = min(MOST, part * group)
    steps = part * group // tile
    vmem = pl.BlockSpec(memory_space=pltpu.VMEM)
    return pl.pallas_call(
        functools.partial(kernel, n, heads, tile),
        out_shape=jax.ShapeDtypeStruct((part, heads * group * hdim), bf16),
        in_specs=[pl.BlockSpec(memory_space=pltpu.SMEM), vmem, vmem, vmem],
        out_specs=vmem,
        scratch_shapes=[
            pltpu.VMEM((12, rows, hdim), bf16),
            pltpu.VMEM((12, rows, hdim), bf16),
            pltpu.VMEM((12, rows, 128), bf16),
            pltpu.VMEM((rows * group, hdim + 128), bf16),
            pltpu.VMEM((rows * group, hdim + 128), f32),
            pltpu.VMEM((rows * group, 128), f32),
            pltpu.VMEM((tile, hdim), f32),
            pltpu.VMEM((heads - 1, part, group * hdim), bf16),
            pltpu.SemaphoreType.DMA((11, 2)),
            pltpu.SemaphoreType.DMA((12, 2)),
            pltpu.SemaphoreType.DMA((heads - 1, steps)),
            pltpu.SemaphoreType.DMA((heads - 1, steps)),
        ],
        compiler_params=pltpu.CompilerParams(
            collective_id=0, has_side_effects=True, vmem_limit_bytes=56 * 1024 * 1024),
    )(doc_lengths, queries.reshape(rows * group, hdim), keys.reshape(rows, hdim), values.reshape(rows, hdim))


def solution(mesh):
    placed = (P("ctx", "head", None), P("ctx", "head", None), P("ctx", "head", None), P())
    return jax.shard_map(
        functools.partial(on_device, mesh), mesh=mesh, in_specs=placed,
        out_specs=P(("ctx", "head"), None), check_vma=False
    )
```

profile of v0, /device:TPU:25, one launch (start us, length us, event | category | flops | bytes accessed | tf_op | source)
XLA Modules:
  0.0 55.5 jit_solution(3998801561355081320)
XLA Ops:
  0.0 53.2 %shard_map.46 = bf16[256,2048]{1,0:T(8,128)(2,1)} custom-call(s32[32]{0:T(128)} %lens_ref.1, bf16[4096,128]{1,0:T(8,128)(2,1)} %bitcast.3, bf16[512,128]{1,0:T(8,128)(2,1)} %bitcast.4, bf16[512,128]{1,0:T(8,128)(2,1)} %bitcast.5), custom_call_target="tpu_custom_call" | custom-call | tf_op jit(solution)/shard_map/pallas_call | solution.py:304
  53.2 2.3 %copy.6 = bf16[256,2048]{1,0:T(8,128)(2,1)} copy(bf16[256,2048]{1,0:T(8,128)(2,1)} %shard_map.46) | data formatting | bytes 2097152
where the time goes:
time: 55.8 us; the launch traced here: 55.5 us
  Pallas kernels  53.2 us (95%)
  local copies, waits for them, and re-layouts  2.3 us (4%)
    pallas_call x1, Pallas kernels, on_device(): pl.pallas_call(functools.partial(kernel, n, heads, tile), out_shape=jax.S...  53.2 us
    unnamed x1, local copies, waits for them, and re-layouts  2.3 us

commit v1 on v0

--- a/solution.py
+++ b/solution.py
@@ -127,13 +127,19 @@
         return (position >= first_row) & (position < end_row)
 
     base = me * rows
+    part = rows // heads
+    tokens = tile // group
+    steps = part // tokens
+    chunk = max(128, tokens)
+
+    def by_token(width, dim):
+        return lax.broadcasted_iota(jnp.int32, (tokens, group, width), dim).reshape(tile, width)
 
     @pl.loop(0, total_rows // tile)
     def _(t):
         at = pl.ds(pl.multiple_of(t * tile, tile), tile)
-        token = (t * tile + lax.broadcasted_iota(jnp.int32, (tile, 128), 0)) // group
         qaug[at, 0:hdim] = q_ref[at, :]
-        qaug[at, hdim:] = jnp.where(member(base + token), 1.0, 0.0).astype(jnp.bfloat16)
+        qaug[at, hdim:] = jnp.where(member(base + t * tokens + by_token(128, 0)), 1.0, 0.0).astype(jnp.bfloat16)
 
     @pl.loop(0, 12)
     def _(s):
@@ -157,17 +163,29 @@
             qaug[at, :], jnp.concatenate([keys, docs], axis=1), (((1,), (1,)), ((), ())),
             preferred_element_type=jnp.float32) * scale
 
-    @pl.loop(0, total_rows // tile)
-    def _(t):
-        at = pl.ds(pl.multiple_of(t * tile, tile), tile)
-        s = score(at, k_ref[...], kdoc[8 + pos])
-        token = (t * tile + lax.broadcasted_iota(jnp.int32, (tile, rows), 0)) // group
-        s = jnp.where(lax.broadcasted_iota(jnp.int32, (tile, rows), 1) <= token, s, -BIG)
-        m = jnp.broadcast_to(jnp.max(s, axis=1, keepdims=True), (tile, 128))
-        e = jnp.exp2(s - spread(m, rows))
-        top[at, :] = m
-        acc[at, 0:128] = jnp.dot(e.astype(jnp.bfloat16), v_ref[...], preferred_element_type=jnp.float32)
-        acc[at, 128:] = sum(e[:, k * 128:(k + 1) * 128] for k in range(rows // 128))
+    def spot(owner, t):
+        return pl.multiple_of(owner * (part * group) + t * tile, tile)
+
+    def diagonal(owner, t):
+        at = pl.ds(spot(owner, t), tile)
+        token = owner * part + t * tokens
+        reach = (token + tokens + chunk - 1) // chunk
+
+        def upto(k):
+            width = k * chunk
+            s = score(at, k_ref[0:width, :], kdoc[8 + pos, 0:width, :])
+            edge = by_token(chunk, 2) - by_token(chunk, 0) <= token - (width - chunk)
+            last = jnp.where(edge, s[:, width - chunk:], -BIG)
+            s = last if k == 1 else jnp.concatenate([s[:, :width - chunk], last], axis=1)
+            m = jnp.broadcast_to(jnp.max(s, axis=1, keepdims=True), (tile, 128))
+            e = jnp.exp2(s - spread(m, width))
+            top[at, :] = m
+            acc[at, 0:128] = jnp.dot(
+                e.astype(jnp.bfloat16), v_ref[0:width, :], preferred_element_type=jnp.float32)
+            acc[at, 128:] = sum(e[:, i * 128:(i + 1) * 128] for i in range(width // 128))
+
+        for k in range(1, rows // chunk + 1):
+            pl.when(reach == k)(functools.partial(upto, k))
 
     def both(at, a, b):
         sa = score(at, kbuf[a], kdoc[a])
@@ -186,14 +204,6 @@
         tot = sum(ea[:, k * 128:(k + 1) * 128] + eb[:, k * 128:(k + 1) * 128] for k in range(rows // 128))
         return jnp.concatenate([acc[at, 0:128] * factor + grown, acc[at, 128:] * factor + tot], axis=1)
 
-    def pair(a, b, valid):
-        @pl.when(valid)
-        def _():
-            @pl.loop(0, total_rows // tile)
-            def _(t):
-                at = pl.ds(pl.multiple_of(t * tile, tile), tile)
-                acc[at, :] = both(at, a, b)
-
     def pick(if_right, if_left):
         return col * if_right + (1 - col) * if_left
 
@@ -201,6 +211,66 @@
     g2 = (4 + pos_x, 4 + pos_d)
     g3 = (pick(8 + pos_x, pos_x), pick(8 + pos_d, pos_d))
     g4 = (pos, core * (8 + pos_m) + (1 - core) * pos_m)
+    pairs = (
+        (pick(g3[0], g1[0]), pick(g3[1], g1[1]), right | has1),
+        (pick(g1[0], g2[0]), pick(g1[1], g2[1]), has1),
+        (pick(g2[0], g4[0]), pick(g2[1], g4[1]), (right & has1) | (leftc & (has2 | (core == 1)))),
+        (pick(g4[0], g3[0]), pick(g4[1], g3[1]), has2 | (right & (core == 1))),
+    )
+    last_a, last_b, last_valid = pairs[3]
+    peers = (heads - 1) * steps
+
+    def peer(u):
+        return (mine + 1 + u // steps) % heads, u % steps
+
+    def pair(a, b, valid, count, place):
+        @pl.when(valid)
+        def _():
+            @pl.loop(0, count)
+            def _(u):
+                at = pl.ds(spot(*place(u)), tile)
+                acc[at, :] = both(at, a, b)
+
+    def local(t):
+        return pl.ds(pl.multiple_of(t * tokens, tokens), tokens)
+
+    def finish(owner, t, own):
+        at = pl.ds(spot(owner, t), tile)
+
+        def close(whole):
+            norm[...] = whole[:, 0:hdim] / jnp.sum(whole[:, hdim:], axis=1, keepdims=True)
+
+        @pl.when(last_valid)
+        def _():
+            close(both(at, last_a, last_b))
+
+        @pl.when(jnp.logical_not(last_valid))
+        def _():
+            close(acc[at, :])
+
+        for g in range(group):
+            piece = norm[pl.ds(g, tokens, stride=group), :].astype(jnp.bfloat16)
+            if own is None:
+                where = pl.ds(pl.multiple_of(mine * (group * hdim) + g * hdim, hdim), hdim)
+                out_ref[local(t), where] = piece
+            else:
+                stage[own, local(t), g * hdim:(g + 1) * hdim] = piece
+
+    columns = pl.ds(pl.multiple_of(mine * (group * hdim), group * hdim), group * hdim)
+
+    def outgoing(d, t):
+        return pltpu.make_async_remote_copy(
+            src_ref=stage.at[d - 1, local(t)],
+            dst_ref=out_ref.at[local(t), columns],
+            send_sem=osend_sem.at[d - 1, t],
+            recv_sem=orecv_sem.at[d - 1, t],
+            device_id={"head": (mine + d) % heads},
+            device_id_type=MESH,
+        )
+
+    @pl.loop(0, peers)
+    def _(u):
+        diagonal(*peer(u))
 
     landed(4 + pos, has1)
     start("Z1")
@@ -211,7 +281,11 @@
     landed(8 + pos_m, None)
     landed(4 + pos_m, has1)
     landed(8 + pos_d, right)
-    pair(pick(g3[0], g1[0]), pick(g3[1], g1[1]), right | has1)
+    pair(*pairs[0], peers, peer)
+
+    @pl.loop(0, steps)
+    def _(t):
+        diagonal(mine, t)
 
     landed(pos, has2)
     start("X2")
@@ -219,54 +293,14 @@
     landed(4 + pos_x, has1)
     start("D1x")
     landed(4 + pos_d, has1)
-    pair(pick(g1[0], g2[0]), pick(g1[1], g2[1]), has1)
+    pair(*pairs[1], peers, peer)
 
     landed(pos_m, has2)
-    pair(pick(g2[0], g4[0]), pick(g2[1], g4[1]), (right & has1) | (leftc & (has2 | (core == 1))))
+    pair(*pairs[2], peers, peer)
 
     landed(pos_x, has2 & leftc)
     start("D2x")
     landed(pos_d, has2 & leftc)
-    last_a, last_b = pick(g4[0], g3[0]), pick(g4[1], g3[1])
-    last_valid = has2 | (right & (core == 1))
-
-    part = rows // heads
-    tokens = tile // group
-    steps = part // tokens
-    columns = pl.ds(pl.multiple_of(mine * (group * hdim), group * hdim), group * hdim)
-
-    def finish(owner, t, own):
-        at = pl.ds(pl.multiple_of(owner * (part * group) + t * tile, tile), tile)
-
-        @pl.when(last_valid)
-        def _():
-            whole = both(at, last_a, last_b)
-            norm[...] = whole[:, 0:hdim] / jnp.sum(whole[:, hdim:], axis=1, keepdims=True)
-
-        @pl.when(jnp.logical_not(last_valid))
-        def _():
-            whole = acc[at, :]
-            norm[...] = whole[:, 0:hdim] / jnp.sum(whole[:, hdim:], axis=1, keepdims=True)
-
-        local = pl.ds(pl.multiple_of(t * tokens, tokens), tokens)
-        for g in range(group):
-            piece = norm[pl.ds(g, tokens, stride=group), :].astype(jnp.bfloat16)
-            if own is None:
-                where = pl.ds(pl.multiple_of(mine * (group * hdim) + g * hdim, hdim), hdim)
-                out_ref[local, where] = piece
-            else:
-                stage[own, local, g * hdim:(g + 1) * hdim] = piece
-
-    def outgoing(d, t):
-        local = pl.ds(pl.multiple_of(t * tokens, tokens), tokens)
-        return pltpu.make_async_remote_copy(
-            src_ref=stage.at[d - 1, local],
-            dst_ref=out_ref.at[local, columns],
-            send_sem=osend_sem.at[d - 1, t],
-            recv_sem=orecv_sem.at[d - 1, t],
-            device_id={"head": (mine + d) % heads},
-            device_id_type=MESH,
-        )
 
     for d in range(1, heads):
         @pl.loop(0, steps)
@@ -274,6 +308,13 @@
             finish((mine + d) % heads, t, d - 1)
             outgoing(d, t).start()
 
+    def choose(p, k):
+        return sum((p == i) * jnp.asarray(pairs[i][k], jnp.int32) for i in range(3))
+
+    @pl.loop(0, 3)
+    def _(p):
+        pair(choose(p, 0), choose(p, 1), choose(p, 2) == 1, steps, lambda t: (mine, t))
+
     @pl.loop(0, steps)
     def _(t):
         finish(mine, t, None)
@@ -283,9 +324,8 @@
         def _(t):
             outgoing(d, t).wait_send()
             source = (mine + heads - d) % heads
-            local = pl.ds(pl.multiple_of(t * tokens, tokens), tokens)
             cols = pl.ds(pl.multiple_of(source * (group * hdim), group * hdim), group * hdim)
-            got = out_ref.at[local, cols]
+            got = out_ref.at[local(t), cols]
             pltpu.make_async_copy(got, got, orecv_sem.at[d - 1, t]).wait()
 
     for name in moves:

time: 55.8 us -> 49.4 us (0.89)
  the two profiles are of different devices: /device:TPU:25 before, /device:TPU:21 now
where the time goes in v1:
time: 49.4 us; the launch traced here: 49.2 us
  Pallas kernels  46.9 us (95%)
  local copies, waits for them, and re-layouts  2.3 us (5%)
    pallas_call x1, Pallas kernels, on_device(): pl.pallas_call(functools.partial(kernel, n, heads, tile), out_shape=jax.S...  46.9 us
    unnamed x1, local copies, waits for them, and re-layouts  2.3 us

profile of v1, /device:TPU:21, one launch (start us, length us, event | category | flops | bytes accessed | tf_op | source)
XLA Modules:
  0.0 49.2 jit_solution(16863245822844985129)
XLA Ops:
  0.0 46.9 %shard_map.46 = bf16[256,2048]{1,0:T(8,128)(2,1)} custom-call(s32[32]{0:T(128)} %lens_ref.1, bf16[4096,128]{1,0:T(8,128)(2,1)} %bitcast.3, bf16[512,128]{1,0:T(8,128)(2,1)} %bitcast.4, bf16[512,128]{1,0:T(8,128)(2,1)} %bitcast.5), custom_call_target="tpu_custom_call" | custom-call | tf_op jit(solution)/shard_map/pallas_call | solution.py:344
  46.9 2.3 %copy.6 = bf16[256,2048]{1,0:T(8,128)(2,1)} copy(bf16[256,2048]{1,0:T(8,128)(2,1)} %shard_map.46) | data formatting | bytes 2097152

commit v2 on v1

v2 whole, which is shorter than its diff:
```python
import functools
import math

import jax
import jax.numpy as jnp
from jax import lax
from jax.experimental import pallas as pl
from jax.experimental.pallas import tpu as pltpu
from jax.sharding import PartitionSpec as P

MESH = pl.DeviceIdType.MESH
BIG = 1e30
MOST = 512
BAND = 128
ORDER = (0, 4, 1, 5, 2, 3, 6, 7)


def kernel(n, heads, tile, lens_ref, q_ref, k_ref, v_ref, out_ref,
           kbuf, vbuf, kdoc, qaug, acc, top, norm, stage,
           send_sem, recv_sem, osend_sem, orecv_sem, load_sem):
    rows, hdim = k_ref.shape
    total_rows = q_ref.shape[0]
    group = total_rows // rows
    me = lax.axis_index("ctx")
    mine = lax.axis_index("head")
    pos = me % 4
    core = pos % 2
    col = pos // 2
    mate = me + 1 - 2 * core
    across = me + 2 - 4 * col
    pos_m = pos + 1 - 2 * core
    pos_x = pos + 2 - 4 * col
    pos_d = pos_x + pos_m - pos
    has1 = me >= 4
    has2 = me >= 8
    feeds = me + 4 < n
    right = col == 1
    leftc = col == 0

    loads = (
        pltpu.make_async_copy(k_ref, kbuf.at[8 + pos], load_sem.at[0]),
        pltpu.make_async_copy(q_ref, qaug.at[:, 0:hdim], load_sem.at[1]),
        pltpu.make_async_copy(v_ref, vbuf.at[8 + pos], load_sem.at[2]),
    )
    for load in loads:
        load.start()

    barrier = pltpu.get_barrier_semaphore()
    for peer in (mate, across):
        pl.semaphore_signal(barrier, inc=1, device_id={"ctx": peer}, device_id_type=MESH)

    @pl.when(has1)
    def _():
        pl.semaphore_signal(barrier, inc=1, device_id={"ctx": me - 4}, device_id_type=MESH)

    @pl.when(feeds)
    def _():
        pl.semaphore_signal(barrier, inc=1, device_id={"ctx": me + 4}, device_id_type=MESH)

    for d in range(1, heads):
        pl.semaphore_signal(barrier, inc=1, device_id={"head": (mine + d) % heads}, device_id_type=MESH)
    pl.semaphore_wait(barrier, 1 + heads + has1.astype(jnp.int32) + feeds.astype(jnp.int32))

    def copies(lane, slot, to_slot, target):
        made = []
        for w, buf, own in ((0, kbuf, k_ref), (1, vbuf, v_ref)):
            made.append(pltpu.make_async_remote_copy(
                src_ref=own if slot is None else buf.at[slot],
                dst_ref=buf.at[to_slot],
                send_sem=send_sem.at[lane, w],
                recv_sem=recv_sem.at[to_slot, w],
                device_id={"ctx": target},
                device_id_type=MESH,
            ))
        return made

    moves = {
        "D0": (copies(0, None, 8 + pos, mate), None),
        "X0": (copies(1, None, 8 + pos, across), leftc),
        "Z0": (copies(2, None, 4 + pos, me + 4), feeds),
        "D0x": (copies(3, 8 + pos_x, 8 + pos_x, mate), right),
        "D1": (copies(4, 4 + pos, 4 + pos, mate), has1),
        "X1": (copies(5, 4 + pos, 4 + pos, across), has1),
        "Z1": (copies(6, 4 + pos, pos, me + 4), has1 & feeds),
        "D1x": (copies(7, 4 + pos_x, 4 + pos_x, mate), has1),
        "D2": (copies(8, pos, pos, mate), has2),
        "X2": (copies(9, pos, pos, across), has2 & right),
        "D2x": (copies(10, pos_x, pos_x, mate), has2 & leftc),
    }

    def when(cond, fn):
        if cond is None:
            fn()
        else:
            pl.when(cond)(fn)

    def start(*names):
        for name in names:
            made, cond = moves[name]

            def go():
                for copy in made:
                    copy.start()

            when(cond, go)

    def sent(name):
        made, cond = moves[name]

        def go():
            for copy in made:
                copy.wait_send()

        when(cond, go)

    def landed(slot, cond, *names):
        for w, buf in ((0, kbuf), (1, vbuf)):
            def go():
                pltpu.make_async_copy(buf.at[slot], buf.at[slot], recv_sem.at[slot, w]).wait()

            when(cond, go)
            for name in names:
                made, also = moves[name]
                when(also, made[w].start)

    start("Z0", "X0", "D0")

    lane = lax.broadcasted_iota(jnp.int32, (8, 128), 1)
    firsts = jnp.full((8, 128), 2**30, jnp.int32)
    ends = jnp.full((8, 128), 2**30, jnp.int32)
    run = jnp.int32(0)
    for d in range(lens_ref.shape[0]):
        firsts = jnp.where(lane == d, run, firsts)
        run = run + lens_ref[d]
        ends = jnp.where(lane == d, run, ends)
    first_row, end_row = firsts[0:1], ends[0:1]

    def member(position):
        return (position >= first_row) & (position < end_row)

    base = me * rows
    part = rows // heads
    tokens = tile // group
    steps = part // tokens
    span = part * group

    def by_token(width, dim):
        return lax.broadcasted_iota(jnp.int32, (tokens, group, width), dim).reshape(tile, width)

    @pl.loop(0, total_rows // tile)
    def _(t):
        at = pl.ds(pl.multiple_of(t * tile, tile), tile)
        qaug[at, hdim:] = jnp.where(member(base + t * tokens + by_token(128, 0)), 1.0, 0.0).astype(jnp.bfloat16)

    @pl.loop(0, 12)
    def _(s):
        kpos = (me - pos - 8 + s) * rows + lax.broadcasted_iota(jnp.int32, (rows, 128), 0)
        kdoc[s] = jnp.where(member(kpos), 0.0, -BIG).astype(jnp.bfloat16)

    @pl.when(me < 8)
    def _():
        @pl.loop(0, 4)
        def _(s):
            kbuf[s] = jnp.zeros((rows, hdim), jnp.bfloat16)
            vbuf[s] = jnp.zeros((rows, hdim), jnp.bfloat16)

    scale = math.log2(math.e) / hdim**0.5

    def spread(x, width):
        return jnp.concatenate([x] * (width // 128), axis=1)

    def raw(at, slot, width):
        return lax.dot_general(
            qaug[at, :], jnp.concatenate([kbuf[slot, 0:width, :], kdoc[slot, 0:width, :]], axis=1),
            (((1,), (1,)), ((), ())), preferred_element_type=jnp.float32)

    def mixed(weight, slot, width):
        ones = jnp.ones((width, 128), jnp.bfloat16)
        return jnp.dot(weight, jnp.concatenate([vbuf[slot, 0:width, :], ones], axis=1),
                       preferred_element_type=jnp.float32)

    def flow(count, one, two, three):
        scores, weights = {}, {}
        for u in range(count + 2):
            if u >= 2:
                three(u - 2, *weights.pop(u - 2))
            if 1 <= u <= count:
                weights[u - 1] = two(u - 1, scores.pop(u - 1))
            if u < count:
                scores[u] = one(u)

    def diagonal():
        def width(t):
            return -(-(t + 1) * tokens // 128) * 128

        def at(t):
            return pl.ds(t * tile, tile)

        def one(t):
            return raw(at(t), 8 + pos, width(t))

        def two(t, s):
            wide, done = width(t), []
            for r in range(0, tile, BAND):
                here = slice(r, r + BAND)
                x = s[here, :] * scale
                edge = by_token(128, 2)[here] - by_token(128, 0)[here] <= t * tokens - (wide - 128)
                last = jnp.where(edge, x[:, wide - 128:], -BIG)
                x = last if wide == 128 else jnp.concatenate([x[:, :wide - 128], last], axis=1)
                m = jnp.broadcast_to(jnp.max(x, axis=1, keepdims=True), (BAND, 128))
                top[pl.ds(t * tile + r, BAND), :] = m
                done.append(jnp.exp2(x - spread(m, wide)).astype(jnp.bfloat16))
            return (jnp.concatenate(done, axis=0),)

        def three(t, weight):
            acc[at(t), :] = mixed(weight, 8 + pos, width(t))

        flow(total_rows // tile, one, two, three)

    def unit(first, a, b):
        def at(u, r=0, size=tile):
            return pl.ds(pl.multiple_of(first + (u % steps) * tile + r, size), size)

        def slot(u):
            return a if u < steps else b

        def one(u):
            return raw(at(u), slot(u), rows)

        def two(u, s):
            done, factors = [], []
            for r in range(0, tile, BAND):
                x = s[r:r + BAND, :] * scale
                m0 = top[at(u, r, BAND), :]
                m = jnp.maximum(m0, jnp.max(x, axis=1, keepdims=True))
                top[at(u, r, BAND), :] = m
                factors.append(jnp.exp2(m0 - m))
                done.append(jnp.exp2(x - spread(m, rows)).astype(jnp.bfloat16))
            return jnp.concatenate(done, axis=0), jnp.concatenate(factors, axis=0)

        def three(u, weight, factor):
            acc[at(u), :] = acc[at(u), :] * spread(factor, 2 * hdim) + mixed(weight, slot(u), rows)

        flow(2 * steps, one, two, three)

    def pick(if_right, if_left):
        return col * if_right + (1 - col) * if_left

    g1 = (4 + pos, 4 + pos_m)
    g2 = (4 + pos_x, 4 + pos_d)
    g3 = (pick(8 + pos_x, pos_x), pick(8 + pos_d, pos_d))
    g4 = (pos, core * (8 + pos_m) + (1 - core) * pos_m)
    pairs = (
        (pick(g3[0], g1[0]), pick(g3[1], g1[1]), right | has1),
        (pick(g1[0], g2[0]), pick(g1[1], g2[1]), has1),
        (pick(g2[0], g4[0]), pick(g2[1], g4[1]), (right & has1) | (leftc & (has2 | (core == 1)))),
        (pick(g4[0], g3[0]), pick(g4[1], g3[1]), has2 | (right & (core == 1))),
    )

    def local(t):
        return pl.ds(pl.multiple_of(t * tokens, tokens), tokens)

    def finish(first, t, put):
        whole = acc[pl.ds(pl.multiple_of(first + t * tile, tile), tile), :]
        norm[...] = whole[:, 0:hdim] / whole[:, hdim:]
        for g in range(group):
            put(g, norm[pl.ds(g, tokens, stride=group), :].astype(jnp.bfloat16))

    columns = pl.ds(pl.multiple_of(mine * (group * hdim), group * hdim), group * hdim)

    def outgoing(d, t):
        return pltpu.make_async_remote_copy(
            src_ref=stage.at[d - 1, local(t)],
            dst_ref=out_ref.at[local(t), columns],
            send_sem=osend_sem.at[d - 1, t],
            recv_sem=orecv_sem.at[d - 1, t],
            device_id={"head": (mine + d) % heads},
            device_id_type=MESH,
        )

    for load in loads:
        load.wait()
    diagonal()

    def event0():
        landed(4 + pos, has1, "Z1", "X1", "D1")
        landed(8 + pos_x, right, "D0x")
        landed(8 + pos_m, None)
        landed(4 + pos_m, has1)
        landed(8 + pos_d, right)

    def event1():
        landed(pos, has2, "X2", "D2")
        landed(4 + pos_x, has1, "D1x")
        landed(4 + pos_d, has1)

    def event2():
        landed(pos_m, has2)

    def event3():
        landed(pos_x, has2 & leftc, "D2x")
        landed(pos_d, has2 & leftc)

    others = list(range(1, heads))
    order = [(p, d) for p in ORDER for d in (others if p < 4 else [heads])]
    order = [(p % 4, d) for p, d in order]
    events = (event0, event1, event2, event3)

    def choose(index, values):
        return sum((index == i) * jnp.asarray(x, jnp.int32) for i, x in enumerate(values))

    @pl.loop(0, len(order))
    def _(u):
        for p, event in enumerate(events):
            pl.when(u == [x for x, _ in order].index(p))(event)
        p = choose(u, [x for x, _ in order])
        d = choose(u, [x for _, x in order])
        first = (mine + d) % heads * span

        @pl.when(choose(p, [x[2] for x in pairs]) == 1)
        def _():
            unit(first, choose(p, [x[0] for x in pairs]), choose(p, [x[1] for x in pairs]))

        @pl.when((p == 3) & (d < heads))
        def _():
            @pl.loop(0, steps)
            def _(t):
                def put(g, piece):
                    stage[d - 1, local(t), g * hdim:(g + 1) * hdim] = piece

                finish(first, t, put)
                outgoing(d, t).start()

        @pl.when((p == 3) & (d == heads))
        def _():
            @pl.loop(0, steps)
            def _(t):
                def put(g, piece):
                    where = pl.ds(pl.multiple_of(mine * (group * hdim) + g * hdim, hdim), hdim)
                    out_ref[local(t), where] = piece

                finish(first, t, put)

    for d in range(1, heads):
        @pl.loop(0, steps)
        def _(t):
            outgoing(d, t).wait_send()
            source = (mine + heads - d) % heads
            cols = pl.ds(pl.multiple_of(source * (group * hdim), group * hdim), group * hdim)
            got = out_ref.at[local(t), cols]
            pltpu.make_async_copy(got, got, orecv_sem.at[d - 1, t]).wait()

    for name in moves:
        sent(name)


def on_device(mesh, queries, keys, values, doc_lengths):
    rows, group, hdim = queries.shape
    heads = mesh.shape["head"]
    n = mesh.shape["ctx"]
    bf16, f32 = jnp.bfloat16, jnp.float32
    part = rows // heads
    tile = min(MOST, part * group)
    steps = part * group // tile
    vmem = pl.BlockSpec(memory_space=pltpu.VMEM)
    anywhere = pl.BlockSpec(memory_space=pl.ANY)
    return pl.pallas_call(
        functools.partial(kernel, n, heads, tile),
        out_shape=pltpu.VMEM((part, heads * group * hdim), bf16),
        in_specs=[pl.BlockSpec(memory_space=pltpu.SMEM), anywhere, anywhere, anywhere],
        out_specs=vmem,
        scratch_shapes=[
            pltpu.VMEM((12, rows, hdim), bf16),
            pltpu.VMEM((12, rows, hdim), bf16),
            pltpu.VMEM((12, rows, 128), bf16),
            pltpu.VMEM((rows * group, hdim + 128), bf16),
            pltpu.VMEM((rows * group, hdim + 128), f32),
            pltpu.VMEM((rows * group, 128), f32),
            pltpu.VMEM((tile, hdim), f32),
            pltpu.VMEM((heads - 1, part, group * hdim), bf16),
            pltpu.SemaphoreType.DMA((11, 2)),
            pltpu.SemaphoreType.DMA((12, 2)),
            pltpu.SemaphoreType.DMA((heads - 1, steps)),
            pltpu.SemaphoreType.DMA((heads - 1, steps)),
            pltpu.SemaphoreType.DMA((3,)),
        ],
        compiler_params=pltpu.CompilerParams(
            collective_id=0, has_side_effects=True, vmem_limit_bytes=56 * 1024 * 1024),
    )(doc_lengths, queries.reshape(rows * group, hdim), keys.reshape(rows, hdim), values.reshape(rows, hdim))


def solution(mesh):
    placed = (P("ctx", "head", None), P("ctx", "head", None), P("ctx", "head", None), P())
    return jax.shard_map(
        functools.partial(on_device, mesh), mesh=mesh, in_specs=placed,
        out_specs=P(("ctx", "head"), None), check_vma=False
    )
```

time: 49.4 us -> 48.5 us (0.982)
  the two profiles are of different devices: /device:TPU:21 before, /device:TPU:25 now
where the time goes in v2:
time: 48.5 us; the launch traced here: 48.3 us
  Pallas kernels  47.3 us (98%)
  local copies, waits for them, and re-layouts  0.97 us (2%)
    pallas_call x1, Pallas kernels, on_device(): pl.pallas_call(functools.partial(kernel, n, heads, tile), out_shape=pltpu...  47.3 us
    unnamed x1, local copies, waits for them, and re-layouts  0.97 us

profile of v2, /device:TPU:25, one launch (start us, length us, event | category | flops | bytes accessed | tf_op | source)
XLA Modules:
  0.0 48.3 jit_solution(13189634362731310175)
XLA Ops:
  0.0 47.3 %shard_map.46 = bf16[256,2048]{1,0:T(8,128)(2,1)S(1)} custom-call(s32[32]{0:T(128)} %lens_ref.1, bf16[4096,128]{1,0:T(8,128)(2,1)} %bitcast.3, bf16[512,128]{1,0:T(8,128)(2,1)} %bitcast.4, bf16[512,128]{1,0:T(8,128)(2,1)} %bitcast.5), custom_call_target="tpu_custom_call" | custom-call | tf_op jit(solution)/shard_map/pallas_call | solution.py:367
  47.3 1.0 %copy.6 = bf16[256,2048]{1,0:T(8,128)(2,1)} copy(bf16[256,2048]{1,0:T(8,128)(2,1)S(1)} %shard_map.46) | data formatting | bytes 2097152

commit v3 on v2

--- a/solution.py
+++ b/solution.py
@@ -12,7 +12,8 @@
 BIG = 1e30
 MOST = 512
 BAND = 128
-ORDER = (0, 4, 1, 5, 2, 3, 6, 7)
+EDGE = 512
+ORDER = (0, 4, 1, 2, 3, 5, 6, 7)
 
 
 def kernel(n, heads, tile, lens_ref, q_ref, k_ref, v_ref, out_ref,
@@ -113,8 +114,10 @@
 
         when(cond, go)
 
-    def landed(slot, cond, *names):
-        for w, buf in ((0, kbuf), (1, vbuf)):
+    def landed(slot, cond, *names, which=(0, 1)):
+        for w in which:
+            buf = (kbuf, vbuf)[w]
+
             def go():
                 pltpu.make_async_copy(buf.at[slot], buf.at[slot], recv_sem.at[slot, w]).wait()
 
@@ -152,17 +155,11 @@
         at = pl.ds(pl.multiple_of(t * tile, tile), tile)
         qaug[at, hdim:] = jnp.where(member(base + t * tokens + by_token(128, 0)), 1.0, 0.0).astype(jnp.bfloat16)
 
-    @pl.loop(0, 12)
-    def _(s):
+    def mark(s):
         kpos = (me - pos - 8 + s) * rows + lax.broadcasted_iota(jnp.int32, (rows, 128), 0)
         kdoc[s] = jnp.where(member(kpos), 0.0, -BIG).astype(jnp.bfloat16)
 
-    @pl.when(me < 8)
-    def _():
-        @pl.loop(0, 4)
-        def _(s):
-            kbuf[s] = jnp.zeros((rows, hdim), jnp.bfloat16)
-            vbuf[s] = jnp.zeros((rows, hdim), jnp.bfloat16)
+    mark(8 + pos)
 
     scale = math.log2(math.e) / hdim**0.5
 
@@ -217,31 +214,41 @@
 
         flow(total_rows // tile, one, two, three)
 
-    def unit(first, a, b):
-        def at(u, r=0, size=tile):
-            return pl.ds(pl.multiple_of(first + (u % steps) * tile + r, size), size)
-
-        def slot(u):
-            return a if u < steps else b
+    def cuts(extent):
+        if extent < 4 * tile or tile % 256:
+            return [(r, min(tile, extent)) for r in range(0, extent, min(tile, extent))]
+        sizes = [EDGE] + [tile] * ((extent - 2 * EDGE) // tile) + [(extent - 2 * EDGE) % tile] * ((extent - 2 * EDGE) % tile > 0) + [EDGE]
+        return [(sum(sizes[:i]), x) for i, x in enumerate(sizes)]
+
+    def unit(first, a, b, extent):
+        pieces = [(r, size, slot) for r, size in cuts(extent) for slot in (a, b)]
+
+        def at(r, size):
+            return pl.ds(pl.multiple_of(first + r, 128), size)
 
         def one(u):
-            return raw(at(u), slot(u), rows)
+            r, size, slot = pieces[u]
+            return raw(at(r, size), slot, rows)
 
         def two(u, s):
+            start_row, size, _ = pieces[u]
             done, factors = [], []
-            for r in range(0, tile, BAND):
+            for r in range(0, size, BAND):
                 x = s[r:r + BAND, :] * scale
-                m0 = top[at(u, r, BAND), :]
+                here = at(start_row + r, BAND)
+                m0 = top[here, :]
                 m = jnp.maximum(m0, jnp.max(x, axis=1, keepdims=True))
-                top[at(u, r, BAND), :] = m
+                top[here, :] = m
                 factors.append(jnp.exp2(m0 - m))
                 done.append(jnp.exp2(x - spread(m, rows)).astype(jnp.bfloat16))
             return jnp.concatenate(done, axis=0), jnp.concatenate(factors, axis=0)
 
         def three(u, weight, factor):
-            acc[at(u), :] = acc[at(u), :] * spread(factor, 2 * hdim) + mixed(weight, slot(u), rows)
-
-        flow(2 * steps, one, two, three)
+            r, size, slot = pieces[u]
+            here = at(r, size)
+            acc[here, :] = acc[here, :] * spread(factor, 2 * hdim) + mixed(weight, slot, rows)
+
+        flow(len(pieces), one, two, three)
 
     def pick(if_right, if_left):
         return col * if_right + (1 - col) * if_left
@@ -282,6 +289,17 @@
         load.wait()
     diagonal()
 
+    @pl.loop(1, 12)
+    def _(s):
+        mark((8 + pos + s) % 12)
+
+    @pl.when(me < 8)
+    def _():
+        @pl.loop(0, 4)
+        def _(s):
+            kbuf[s] = jnp.zeros((rows, hdim), jnp.bfloat16)
+            vbuf[s] = jnp.zeros((rows, hdim), jnp.bfloat16)
+
     def event0():
         landed(4 + pos, has1, "Z1", "X1", "D1")
         landed(8 + pos_x, right, "D0x")
@@ -290,46 +308,64 @@
         landed(8 + pos_d, right)
 
     def event1():
-        landed(pos, has2, "X2", "D2")
+        landed(pos, has2, "X2", "D2", which=(0,))
+
+    def event2():
+        landed(pos, has2, "X2", "D2", which=(1,))
         landed(4 + pos_x, has1, "D1x")
         landed(4 + pos_d, has1)
 
-    def event2():
+    def event3():
         landed(pos_m, has2)
-
-    def event3():
-        landed(pos_x, has2 & leftc, "D2x")
+        landed(pos_x, has2 & leftc, "D2x", which=(0,))
+
+    def event4():
+        landed(pos_x, has2 & leftc, "D2x", which=(1,))
         landed(pos_d, has2 & leftc)
 
     others = list(range(1, heads))
     order = [(p, d) for p in ORDER for d in (others if p < 4 else [heads])]
     order = [(p % 4, d) for p, d in order]
-    events = (event0, event1, event2, event3)
+    kinds = [p if d < heads else p + 4 for p, d in order]
+    events = ((0, event0), (4, event1), (1, event2), (2, event3), (3, event4))
+    half = span // 2 if steps % 2 == 0 else span
 
     def choose(index, values):
         return sum((index == i) * jnp.asarray(x, jnp.int32) for i, x in enumerate(values))
 
     @pl.loop(0, len(order))
     def _(u):
-        for p, event in enumerate(events):
-            pl.when(u == [x for x, _ in order].index(p))(event)
+        for kind, event in events:
+            pl.when(u == kinds.index(kind))(event)
         p = choose(u, [x for x, _ in order])
         d = choose(u, [x for _, x in order])
         first = (mine + d) % heads * span
 
-        @pl.when(choose(p, [x[2] for x in pairs]) == 1)
+        valid = choose(p, [x[2] for x in pairs]) == 1
+        slots = choose(p, [x[0] for x in pairs]), choose(p, [x[1] for x in pairs])
+        closing = (p == 3) & (d < heads)
+
+        @pl.when(valid & jnp.logical_not(closing))
         def _():
-            unit(first, choose(p, [x[0] for x in pairs]), choose(p, [x[1] for x in pairs]))
-
-        @pl.when((p == 3) & (d < heads))
+            unit(first, *slots, span)
+
+        @pl.when(closing)
         def _():
-            @pl.loop(0, steps)
-            def _(t):
-                def put(g, piece):
-                    stage[d - 1, local(t), g * hdim:(g + 1) * hdim] = piece
-
-                finish(first, t, put)
-                outgoing(d, t).start()
+            @pl.loop(0, span // half)
+            def _(h):
+                @pl.when(valid)
+                def _():
+                    unit(first + h * half, *slots, half)
+
+                @pl.loop(0, half // tile)
+                def _(x):
+                    t = h * (half // tile) + x
+
+                    def put(g, piece):
+                        stage[d - 1, local(t), g * hdim:(g + 1) * hdim] = piece
+
+                    finish(first, t, put)
+                    outgoing(d, t).start()
 
         @pl.when((p == 3) & (d == heads))
         def _():

time: 48.5 us -> 42.1 us (0.87)
  Pallas kernels: 47.3 us -> 40.9 us
    pallas_call x1, Pallas kernels: 47.3 us -> 40.9 us  [on_device(): pl.pallas_call(functools.partial(kernel, n, heads, tile), out_shape=pltpu...]
where the time goes in v3:
time: 42.1 us; the launch traced here: 41.9 us
  Pallas kernels  40.9 us (97%)
  local copies, waits for them, and re-layouts  0.97 us (2%)
    pallas_call x1, Pallas kernels, on_device(): pl.pallas_call(functools.partial(kernel, n, heads, tile), out_shape=pltpu...  40.9 us
    unnamed x1, local copies, waits for them, and re-layouts  0.97 us

profile of v3, /device:TPU:25, one launch (start us, length us, event | category | flops | bytes accessed | tf_op | source)
XLA Modules:
  0.0 41.9 jit_solution(14504600855039128777)
XLA Ops:
  0.0 40.9 %shard_map.46 = bf16[256,2048]{1,0:T(8,128)(2,1)S(1)} custom-call(s32[32]{0:T(128)} %lens_ref.1, bf16[4096,128]{1,0:T(8,128)(2,1)} %bitcast.3, bf16[512,128]{1,0:T(8,128)(2,1)} %bitcast.4, bf16[512,128]{1,0:T(8,128)(2,1)} %bitcast.5), custom_call_target="tpu_custom_call" | custom-call | tf_op jit(solution)/shard_map/pallas_call | solution.py:403
  40.9 1.0 %copy.6 = bf16[256,2048]{1,0:T(8,128)(2,1)} copy(bf16[256,2048]{1,0:T(8,128)(2,1)S(1)} %shard_map.46) | data formatting | bytes 2097152

commit v4 on v3

--- a/solution.py
+++ b/solution.py
@@ -12,8 +12,9 @@
 BIG = 1e30
 MOST = 512
 BAND = 128
-EDGE = 512
-ORDER = (0, 4, 1, 2, 3, 5, 6, 7)
+ORDER = (1, 2, 3, 5, 6, 7)
+LOW, HIGH = (0, 1), (2, 3)
+ALL = LOW + HIGH
 
 
 def kernel(n, heads, tile, lens_ref, q_ref, k_ref, v_ref, out_ref,
@@ -62,18 +63,18 @@
         pl.semaphore_signal(barrier, inc=1, device_id={"head": (mine + d) % heads}, device_id_type=MESH)
     pl.semaphore_wait(barrier, 1 + heads + has1.astype(jnp.int32) + feeds.astype(jnp.int32))
 
+    half_keys = rows // 2
+    parts = [(own, buf, pl.ds(h * half_keys, half_keys)) for h in range(2) for own, buf in ((k_ref, kbuf), (v_ref, vbuf))]
+
     def copies(lane, slot, to_slot, target):
-        made = []
-        for w, buf, own in ((0, kbuf, k_ref), (1, vbuf, v_ref)):
-            made.append(pltpu.make_async_remote_copy(
-                src_ref=own if slot is None else buf.at[slot],
-                dst_ref=buf.at[to_slot],
-                send_sem=send_sem.at[lane, w],
-                recv_sem=recv_sem.at[to_slot, w],
-                device_id={"ctx": target},
-                device_id_type=MESH,
-            ))
-        return made
+        return [pltpu.make_async_remote_copy(
+            src_ref=own.at[where] if slot is None else buf.at[slot, where],
+            dst_ref=buf.at[to_slot, where],
+            send_sem=send_sem.at[lane, w],
+            recv_sem=recv_sem.at[to_slot, w],
+            device_id={"ctx": target},
+            device_id_type=MESH,
+        ) for w, (own, buf, where) in enumerate(parts)]
 
     moves = {
         "D0": (copies(0, None, 8 + pos, mate), None),
@@ -95,16 +96,6 @@
         else:
             pl.when(cond)(fn)
 
-    def start(*names):
-        for name in names:
-            made, cond = moves[name]
-
-            def go():
-                for copy in made:
-                    copy.start()
-
-            when(cond, go)
-
     def sent(name):
         made, cond = moves[name]
 
@@ -114,19 +105,23 @@
 
         when(cond, go)
 
-    def landed(slot, cond, *names, which=(0, 1)):
+    def landed(slot, cond, *names, which=ALL):
         for w in which:
-            buf = (kbuf, vbuf)[w]
+            _, buf, where = parts[w]
 
             def go():
-                pltpu.make_async_copy(buf.at[slot], buf.at[slot], recv_sem.at[slot, w]).wait()
+                spot = buf.at[slot, where]
+                pltpu.make_async_copy(spot, spot, recv_sem.at[slot, w]).wait()
 
             when(cond, go)
             for name in names:
                 made, also = moves[name]
                 when(also, made[w].start)
 
-    start("Z0", "X0", "D0")
+    for w in ALL:
+        for name in ("Z0", "X0", "D0"):
+            made, also = moves[name]
+            when(also, made[w].start)
 
     lane = lax.broadcasted_iota(jnp.int32, (8, 128), 1)
     firsts = jnp.full((8, 128), 2**30, jnp.int32)
@@ -175,6 +170,16 @@
         ones = jnp.ones((width, 128), jnp.bfloat16)
         return jnp.dot(weight, jnp.concatenate([vbuf[slot, 0:width, :], ones], axis=1),
                        preferred_element_type=jnp.float32)
+
+    def raw_pair(at, a, b, where):
+        keys = [jnp.concatenate([kbuf[x, where, :], kdoc[x, where, :]], axis=1) for x in (a, b)]
+        return lax.dot_general(
+            qaug[at, :], jnp.concatenate(keys, axis=0), (((1,), (1,)), ((), ())), preferred_element_type=jnp.float32)
+
+    def mixed_pair(weight, a, b, where):
+        ones = jnp.ones((rows, 128), jnp.bfloat16)
+        vals = jnp.concatenate([vbuf[a, where, :], vbuf[b, where, :]], axis=0)
+        return jnp.dot(weight, jnp.concatenate([vals, ones], axis=1), preferred_element_type=jnp.float32)
 
     def flow(count, one, two, three):
         scores, weights = {}, {}
@@ -214,28 +219,19 @@
 
         flow(total_rows // tile, one, two, three)
 
-    def cuts(extent):
-        if extent < 4 * tile or tile % 256:
-            return [(r, min(tile, extent)) for r in range(0, extent, min(tile, extent))]
-        sizes = [EDGE] + [tile] * ((extent - 2 * EDGE) // tile) + [(extent - 2 * EDGE) % tile] * ((extent - 2 * EDGE) % tile > 0) + [EDGE]
-        return [(sum(sizes[:i]), x) for i, x in enumerate(sizes)]
-
-    def unit(first, a, b, extent):
-        pieces = [(r, size, slot) for r, size in cuts(extent) for slot in (a, b)]
-
+    def work(first, a, b, pieces):
         def at(r, size):
-            return pl.ds(pl.multiple_of(first + r, 128), size)
+            return pl.ds(pl.multiple_of(first + r, BAND), size)
 
         def one(u):
-            r, size, slot = pieces[u]
-            return raw(at(r, size), slot, rows)
+            r, where = pieces[u]
+            return raw_pair(at(r, tile), a, b, where)
 
         def two(u, s):
-            start_row, size, _ = pieces[u]
             done, factors = [], []
-            for r in range(0, size, BAND):
+            for r in range(0, tile, BAND):
                 x = s[r:r + BAND, :] * scale
-                here = at(start_row + r, BAND)
+                here = at(pieces[u][0] + r, BAND)
                 m0 = top[here, :]
                 m = jnp.maximum(m0, jnp.max(x, axis=1, keepdims=True))
                 top[here, :] = m
@@ -244,24 +240,28 @@
             return jnp.concatenate(done, axis=0), jnp.concatenate(factors, axis=0)
 
         def three(u, weight, factor):
-            r, size, slot = pieces[u]
-            here = at(r, size)
-            acc[here, :] = acc[here, :] * spread(factor, 2 * hdim) + mixed(weight, slot, rows)
+            r, where = pieces[u]
+            here = at(r, tile)
+            acc[here, :] = acc[here, :] * spread(factor, 2 * hdim) + mixed_pair(weight, a, b, where)
 
         flow(len(pieces), one, two, three)
+
+    def unit(first, a, b, extent):
+        work(first, a, b, [(r, parts[w][2]) for r in range(0, extent, tile) for w in (0, 2)])
+
+    def sweep(a, b, h):
+        where = pl.ds(pl.multiple_of(h * half_keys, half_keys), half_keys)
+        work(0, a, b, [(r, where) for r in range(0, total_rows, tile)])
 
     def pick(if_right, if_left):
         return col * if_right + (1 - col) * if_left
 
-    g1 = (4 + pos, 4 + pos_m)
-    g2 = (4 + pos_x, 4 + pos_d)
-    g3 = (pick(8 + pos_x, pos_x), pick(8 + pos_d, pos_d))
-    g4 = (pos, core * (8 + pos_m) + (1 - core) * pos_m)
+    near = core * (8 + pos_m) + (1 - core) * pos_m
     pairs = (
-        (pick(g3[0], g1[0]), pick(g3[1], g1[1]), right | has1),
-        (pick(g1[0], g2[0]), pick(g1[1], g2[1]), has1),
-        (pick(g2[0], g4[0]), pick(g2[1], g4[1]), (right & has1) | (leftc & (has2 | (core == 1)))),
-        (pick(g4[0], g3[0]), pick(g4[1], g3[1]), has2 | (right & (core == 1))),
+        (pick(8 + pos_x, 4 + pos), pick(8 + pos_d, 4 + pos_m), right | has1),
+        (pick(4 + pos, 4 + pos_x), pick(4 + pos_m, pos), has1),
+        (pick(4 + pos_x, 4 + pos_d), pick(4 + pos_d, near), has1 | (leftc & (core == 1))),
+        (pick(pos, pos_x), pick(near, pos_d), has2 | (right & (core == 1))),
     )
 
     def local(t):
@@ -289,45 +289,59 @@
         load.wait()
     diagonal()
 
+    def first_in(which):
+        landed(4 + pos, has1, "Z1", "X1", "D1", which=which)
+        landed(8 + pos_x, right, "D0x", which=which)
+
+    def first_over(which):
+        landed(4 + pos_m, has1, which=which)
+        landed(8 + pos_d, right, which=which)
+
+    first_in(LOW)
+
     @pl.loop(1, 12)
     def _(s):
         mark((8 + pos + s) % 12)
 
-    @pl.when(me < 8)
-    def _():
-        @pl.loop(0, 4)
-        def _(s):
-            kbuf[s] = jnp.zeros((rows, hdim), jnp.bfloat16)
-            vbuf[s] = jnp.zeros((rows, hdim), jnp.bfloat16)
-
-    def event0():
-        landed(4 + pos, has1, "Z1", "X1", "D1")
-        landed(8 + pos_x, right, "D0x")
+    @pl.loop(0, 4 * (me < 8).astype(jnp.int32) + 4 * (me < 4).astype(jnp.int32))
+    def _(s):
+        kbuf[s] = jnp.zeros((rows, hdim), jnp.bfloat16)
+        vbuf[s] = jnp.zeros((rows, hdim), jnp.bfloat16)
+
+    first_over(LOW)
+
+    @pl.loop(0, 2)
+    def _(h):
+        @pl.when(h == 1)
+        def _():
+            first_in(HIGH)
+            first_over(HIGH)
+            landed(pos, has2, "X2", "D2", which=LOW)
+            landed(4 + pos_x, has1, "D1x", which=LOW)
+
+        @pl.when(pairs[0][2])
+        def _():
+            sweep(pairs[0][0], pairs[0][1], h)
+
+    def event1():
+        landed(pos, has2, "X2", "D2", which=HIGH)
+        landed(4 + pos_x, has1, "D1x", which=HIGH)
+
+    def event2():
         landed(8 + pos_m, None)
-        landed(4 + pos_m, has1)
-        landed(8 + pos_d, right)
-
-    def event1():
-        landed(pos, has2, "X2", "D2", which=(0,))
-
-    def event2():
-        landed(pos, has2, "X2", "D2", which=(1,))
-        landed(4 + pos_x, has1, "D1x")
         landed(4 + pos_d, has1)
+        landed(pos_m, has2)
+        landed(pos_x, has2 & leftc, "D2x", which=LOW)
 
     def event3():
-        landed(pos_m, has2)
-        landed(pos_x, has2 & leftc, "D2x", which=(0,))
-
-    def event4():
-        landed(pos_x, has2 & leftc, "D2x", which=(1,))
+        landed(pos_x, has2 & leftc, "D2x", which=HIGH)
         landed(pos_d, has2 & leftc)
 
     others = list(range(1, heads))
     order = [(p, d) for p in ORDER for d in (others if p < 4 else [heads])]
     order = [(p % 4, d) for p, d in order]
     kinds = [p if d < heads else p + 4 for p, d in order]
-    events = ((0, event0), (4, event1), (1, event2), (2, event3), (3, event4))
+    events = ((1, event1), (2, event2), (3, event3))
     half = span // 2 if steps % 2 == 0 else span
 
     def choose(index, values):
@@ -414,8 +428,8 @@
             pltpu.VMEM((rows * group, 128), f32),
             pltpu.VMEM((tile, hdim), f32),
             pltpu.VMEM((heads - 1, part, group * hdim), bf16),
-            pltpu.SemaphoreType.DMA((11, 2)),
-            pltpu.SemaphoreType.DMA((12, 2)),
+            pltpu.SemaphoreType.DMA((11, 4)),
+            pltpu.SemaphoreType.DMA((12, 4)),
             pltpu.SemaphoreType.DMA((heads - 1, steps)),
             pltpu.SemaphoreType.DMA((heads - 1, steps)),
             pltpu.SemaphoreType.DMA((3,)),

time: 42.1 us -> 41.8 us (level)
  Pallas kernels: 40.9 us -> 40.3 us
    pallas_call x1, Pallas kernels: 40.9 us -> 40.3 us  [on_device(): pl.pallas_call(functools.partial(kernel, n, heads, tile), out_shape=pltpu...]
where the time goes in v4:
time: 41.8 us; the launch traced here: 41.3 us
  Pallas kernels  40.3 us (96%)
  local copies, waits for them, and re-layouts  0.97 us (2%)
    pallas_call x1, Pallas kernels, on_device(): pl.pallas_call(functools.partial(kernel, n, heads, tile), out_shape=pltpu...  40.3 us
    unnamed x1, local copies, waits for them, and re-layouts  0.97 us

profile of v4, /device:TPU:25, one launch (start us, length us, event | category | flops | bytes accessed | tf_op | source)
XLA Modules:
  0.0 41.3 jit_solution(2012040546511282584)
XLA Ops:
  0.0 40.3 %shard_map.46 = bf16[256,2048]{1,0:T(8,128)(2,1)S(1)} custom-call(s32[32]{0:T(128)} %lens_ref.1, bf16[4096,128]{1,0:T(8,128)(2,1)} %bitcast.3, bf16[512,128]{1,0:T(8,128)(2,1)} %bitcast.4, bf16[512,128]{1,0:T(8,128)(2,1)} %bitcast.5), custom_call_target="tpu_custom_call" | custom-call | tf_op jit(solution)/shard_map/pallas_call | solution.py:417
  40.3 1.0 %copy.6 = bf16[256,2048]{1,0:T(8,128)(2,1)} copy(bf16[256,2048]{1,0:T(8,128)(2,1)S(1)} %shard_map.46) | data formatting | bytes 2097152

commit v5 on v4

--- a/solution.py
+++ b/solution.py
@@ -17,9 +17,9 @@
 ALL = LOW + HIGH
 
 
-def kernel(n, heads, tile, lens_ref, q_ref, k_ref, v_ref, out_ref,
+def kernel(n, heads, tile, lens_in, q_ref, k_ref, v_ref, out_ref,
            kbuf, vbuf, kdoc, qaug, acc, top, norm, stage,
-           send_sem, recv_sem, osend_sem, orecv_sem, load_sem):
+           lens_ref, send_sem, recv_sem, osend_sem, orecv_sem, load_sem):
     rows, hdim = k_ref.shape
     total_rows = q_ref.shape[0]
     group = total_rows // rows
@@ -39,6 +39,8 @@
     right = col == 1
     leftc = col == 0
 
+    lens_load = pltpu.make_async_copy(lens_in, lens_ref, load_sem.at[3])
+    lens_load.start()
     loads = (
         pltpu.make_async_copy(k_ref, kbuf.at[8 + pos], load_sem.at[0]),
         pltpu.make_async_copy(q_ref, qaug.at[:, 0:hdim], load_sem.at[1]),
@@ -61,7 +63,6 @@
 
     for d in range(1, heads):
         pl.semaphore_signal(barrier, inc=1, device_id={"head": (mine + d) % heads}, device_id_type=MESH)
-    pl.semaphore_wait(barrier, 1 + heads + has1.astype(jnp.int32) + feeds.astype(jnp.int32))
 
     half_keys = rows // 2
     parts = [(own, buf, pl.ds(h * half_keys, half_keys)) for h in range(2) for own, buf in ((k_ref, kbuf), (v_ref, vbuf))]
@@ -118,10 +119,13 @@
                 made, also = moves[name]
                 when(also, made[w].start)
 
-    for w in ALL:
-        for name in ("Z0", "X0", "D0"):
-            made, also = moves[name]
-            when(also, made[w].start)
+    def begin(which):
+        for w in which:
+            for name in ("Z0", "X0", "D0"):
+                made, also = moves[name]
+                when(also, made[w].start)
+
+    lens_load.wait()
 
     lane = lax.broadcasted_iota(jnp.int32, (8, 128), 1)
     firsts = jnp.full((8, 128), 2**30, jnp.int32)
@@ -155,6 +159,8 @@
         kdoc[s] = jnp.where(member(kpos), 0.0, -BIG).astype(jnp.bfloat16)
 
     mark(8 + pos)
+    pl.semaphore_wait(barrier, 1 + heads + has1.astype(jnp.int32) + feeds.astype(jnp.int32))
+    begin(LOW)
 
     scale = math.log2(math.e) / hdim**0.5
 
@@ -288,6 +294,7 @@
     for load in loads:
         load.wait()
     diagonal()
+    begin(HIGH)
 
     def first_in(which):
         landed(4 + pos, has1, "Z1", "X1", "D1", which=which)
@@ -334,7 +341,6 @@
         landed(pos_x, has2 & leftc, "D2x", which=LOW)
 
     def event3():
-        landed(pos_x, has2 & leftc, "D2x", which=HIGH)
         landed(pos_d, has2 & leftc)
 
     others = list(range(1, heads))
@@ -357,7 +363,7 @@
 
         valid = choose(p, [x[2] for x in pairs]) == 1
         slots = choose(p, [x[0] for x in pairs]), choose(p, [x[1] for x in pairs])
-        closing = (p == 3) & (d < heads)
+        closing = (p >= 2) & (d < heads)
 
         @pl.when(valid & jnp.logical_not(closing))
         def _():
@@ -367,11 +373,15 @@
         def _():
             @pl.loop(0, span // half)
             def _(h):
+                @pl.when((u == kinds.index(2)) & (h == span // half - 1))
+                def _():
+                    landed(pos_x, has2 & leftc, "D2x", which=HIGH)
+
                 @pl.when(valid)
                 def _():
                     unit(first + h * half, *slots, half)
 
-                @pl.loop(0, half // tile)
+                @pl.loop(0, jnp.where(p == 3, half // tile, 0))
                 def _(x):
                     t = h * (half // tile) + x
 
@@ -417,7 +427,7 @@
     return pl.pallas_call(
         functools.partial(kernel, n, heads, tile),
         out_shape=pltpu.VMEM((part, heads * group * hdim), bf16),
-        in_specs=[pl.BlockSpec(memory_space=pltpu.SMEM), anywhere, anywhere, anywhere],
+        in_specs=[anywhere] * 4,
         out_specs=vmem,
         scratch_shapes=[
             pltpu.VMEM((12, rows, hdim), bf16),
@@ -428,11 +438,12 @@
             pltpu.VMEM((rows * group, 128), f32),
             pltpu.VMEM((tile, hdim), f32),
             pltpu.VMEM((heads - 1, part, group * hdim), bf16),
+            pltpu.SMEM(doc_lengths.shape, jnp.int32),
             pltpu.SemaphoreType.DMA((11, 4)),
             pltpu.SemaphoreType.DMA((12, 4)),
             pltpu.SemaphoreType.DMA((heads - 1, steps)),
             pltpu.SemaphoreType.DMA((heads - 1, steps)),
-            pltpu.SemaphoreType.DMA((3,)),
+            pltpu.SemaphoreType.DMA((4,)),
         ],
         compiler_params=pltpu.CompilerParams(
             collective_id=0, has_side_effects=True, vmem_limit_bytes=56 * 1024 * 1024),

time: 41.8 us -> 40.4 us (0.967)
  Pallas kernels: 40.3 us -> 38.9 us
    pallas_call x1, Pallas kernels: 40.3 us -> 38.9 us  [on_device(): pl.pallas_call(functools.partial(kernel, n, heads, tile), out_shape=pltpu...]
where the time goes in v5:
time: 40.4 us; the launch traced here: 39.9 us
  Pallas kernels  38.9 us (96%)
  local copies, waits for them, and re-layouts  0.97 us (2%)
    pallas_call x1, Pallas kernels, on_device(): pl.pallas_call(functools.partial(kernel, n, heads, tile), out_shape=pltpu...  38.9 us
    unnamed x1, local copies, waits for them, and re-layouts  0.97 us

profile of v5, /device:TPU:25, one launch (start us, length us, event | category | flops | bytes accessed | tf_op | source)
XLA Modules:
  0.0 39.9 jit_solution(15146066704628020967)
XLA Ops:
  0.0 38.9 %shard_map.46 = bf16[256,2048]{1,0:T(8,128)(2,1)S(1)} custom-call(s32[32]{0:T(128)} %lens_in.1, bf16[4096,128]{1,0:T(8,128)(2,1)} %bitcast.3, bf16[512,128]{1,0:T(8,128)(2,1)} %bitcast.4, bf16[512,128]{1,0:T(8,128)(2,1)} %bitcast.5), custom_call_target="tpu_custom_call" | custom-call | tf_op jit(solution)/shard_map/pallas_call | solution.py:427
  38.9 1.0 %copy.6 = bf16[256,2048]{1,0:T(8,128)(2,1)} copy(bf16[256,2048]{1,0:T(8,128)(2,1)S(1)} %shard_map.46) | data formatting | bytes 2097152

commit v6 on v5

--- a/solution.py
+++ b/solution.py
@@ -145,6 +145,7 @@
     tokens = tile // group
     steps = part // tokens
     span = part * group
+    swath = total_rows // 2
 
     def by_token(width, dim):
         return lax.broadcasted_iota(jnp.int32, (tokens, group, width), dim).reshape(tile, width)
@@ -255,9 +256,9 @@
     def unit(first, a, b, extent):
         work(first, a, b, [(r, parts[w][2]) for r in range(0, extent, tile) for w in (0, 2)])
 
-    def sweep(a, b, h):
+    def sweep(first, a, b, h):
         where = pl.ds(pl.multiple_of(h * half_keys, half_keys), half_keys)
-        work(0, a, b, [(r, where) for r in range(0, total_rows, tile)])
+        work(first, a, b, [(r, where) for r in range(0, swath, tile)])
 
     def pick(if_right, if_left):
         return col * if_right + (1 - col) * if_left
@@ -317,18 +318,24 @@
 
     first_over(LOW)
 
-    @pl.loop(0, 2)
-    def _(h):
-        @pl.when(h == 1)
+    @pl.loop(0, 4)
+    def _(i):
+        @pl.when(i == 1)
         def _():
             first_in(HIGH)
+
+        @pl.when(i == 2)
+        def _():
             first_over(HIGH)
+
+        @pl.when(i == 3)
+        def _():
             landed(pos, has2, "X2", "D2", which=LOW)
             landed(4 + pos_x, has1, "D1x", which=LOW)
 
         @pl.when(pairs[0][2])
         def _():
-            sweep(pairs[0][0], pairs[0][1], h)
+            sweep(i % 2 * swath, pairs[0][0], pairs[0][1], i // 2)
 
     def event1():
         landed(pos, has2, "X2", "D2", which=HIGH)

time: 40.4 us -> 40.1 us (level)
    pallas_call x1, Pallas kernels: 38.9 us -> 38.5 us  [on_device(): pl.pallas_call(functools.partial(kernel, n, heads, tile), out_shape=pltpu...]
where the time goes in v6:
time: 40.1 us; the launch traced here: 39.4 us
  Pallas kernels  38.5 us (96%)
  local copies, waits for them, and re-layouts  0.97 us (2%)
    pallas_call x1, Pallas kernels, on_device(): pl.pallas_call(functools.partial(kernel, n, heads, tile), out_shape=pltpu...  38.5 us
    unnamed x1, local copies, waits for them, and re-layouts  0.97 us

profile of v6, /device:TPU:25, one launch (start us, length us, event | category | flops | bytes accessed | tf_op | source)
XLA Modules:
  0.0 39.4 jit_solution(2381073154098494408)
XLA Ops:
  0.0 38.5 %shard_map.46 = bf16[256,2048]{1,0:T(8,128)(2,1)S(1)} custom-call(s32[32]{0:T(128)} %lens_in.1, bf16[4096,128]{1,0:T(8,128)(2,1)} %bitcast.3, bf16[512,128]{1,0:T(8,128)(2,1)} %bitcast.4, bf16[512,128]{1,0:T(8,128)(2,1)} %bitcast.5), custom_call_target="tpu_custom_call" | custom-call | tf_op jit(solution)/shard_map/pallas_call | solution.py:434
  38.5 1.0 %copy.6 = bf16[256,2048]{1,0:T(8,128)(2,1)} copy(bf16[256,2048]{1,0:T(8,128)(2,1)S(1)} %shard_map.46) | data formatting | bytes 2097152

commit v7 on v6

--- a/solution.py
+++ b/solution.py
@@ -305,8 +305,6 @@
         landed(4 + pos_m, has1, which=which)
         landed(8 + pos_d, right, which=which)
 
-    first_in(LOW)
-
     @pl.loop(1, 12)
     def _(s):
         mark((8 + pos + s) % 12)
@@ -316,6 +314,7 @@
         kbuf[s] = jnp.zeros((rows, hdim), jnp.bfloat16)
         vbuf[s] = jnp.zeros((rows, hdim), jnp.bfloat16)
 
+    first_in(LOW)
     first_over(LOW)
 
     @pl.loop(0, 4)
@@ -348,6 +347,7 @@
         landed(pos_x, has2 & leftc, "D2x", which=LOW)
 
     def event3():
+        landed(pos_x, has2 & leftc, "D2x", which=HIGH)
         landed(pos_d, has2 & leftc)
 
     others = list(range(1, heads))
@@ -355,7 +355,6 @@
     order = [(p % 4, d) for p, d in order]
     kinds = [p if d < heads else p + 4 for p, d in order]
     events = ((1, event1), (2, event2), (3, event3))
-    half = span // 2 if steps % 2 == 0 else span
 
     def choose(index, values):
         return sum((index == i) * jnp.asarray(x, jnp.int32) for i, x in enumerate(values))
@@ -370,7 +369,7 @@
 
         valid = choose(p, [x[2] for x in pairs]) == 1
         slots = choose(p, [x[0] for x in pairs]), choose(p, [x[1] for x in pairs])
-        closing = (p >= 2) & (d < heads)
+        closing = (p == 3) & (d < heads)
 
         @pl.when(valid & jnp.logical_not(closing))
         def _():
@@ -378,25 +377,17 @@
 
         @pl.when(closing)
         def _():
-            @pl.loop(0, span // half)
-            def _(h):
-                @pl.when((u == kinds.index(2)) & (h == span // half - 1))
-                def _():
-                    landed(pos_x, has2 & leftc, "D2x", which=HIGH)
-
+            @pl.loop(0, steps)
+            def _(t):
                 @pl.when(valid)
                 def _():
-                    unit(first + h * half, *slots, half)
-
-                @pl.loop(0, jnp.where(p == 3, half // tile, 0))
-                def _(x):
-                    t = h * (half // tile) + x
-
-                    def put(g, piece):
-                        stage[d - 1, local(t), g * hdim:(g + 1) * hdim] = piece
-
-                    finish(first, t, put)
-                    outgoing(d, t).start()
+                    unit(first + t * tile, *slots, tile)
+
+                def put(g, piece):
+                    stage[d - 1, local(t), g * hdim:(g + 1) * hdim] = piece
+
+                finish(first, t, put)
+                outgoing(d, t).start()
 
         @pl.when((p == 3) & (d == heads))
         def _():

time: 40.1 us -> 39.6 us (0.988); the launches traced: 39.4 us -> 39.5 us
  no operation moved by 1% of the time
where the time goes in v7:
time: 39.6 us; the launch traced here: 39.5 us
  Pallas kernels  38.5 us (97%)
  local copies, waits for them, and re-layouts  0.97 us (2%)
    pallas_call x1, Pallas kernels, on_device(): pl.pallas_call(functools.partial(kernel, n, heads, tile), out_shape=pltpu...  38.5 us
    unnamed x1, local copies, waits for them, and re-layouts  0.97 us

profile of v7, /device:TPU:25, one launch (start us, length us, event | category | flops | bytes accessed | tf_op | source)
XLA Modules:
  0.0 39.5 jit_solution(7515992134169027019)
XLA Ops:
  0.0 38.5 %shard_map.46 = bf16[256,2048]{1,0:T(8,128)(2,1)S(1)} custom-call(s32[32]{0:T(128)} %lens_in.1, bf16[4096,128]{1,0:T(8,128)(2,1)} %bitcast.3, bf16[512,128]{1,0:T(8,128)(2,1)} %bitcast.4, bf16[512,128]{1,0:T(8,128)(2,1)} %bitcast.5), custom_call_target="tpu_custom_call" | custom-call | tf_op jit(solution)/shard_map/pallas_call | solution.py:425
  38.5 1.0 %copy.6 = bf16[256,2048]{1,0:T(8,128)(2,1)} copy(bf16[256,2048]{1,0:T(8,128)(2,1)S(1)} %shard_map.46) | data formatting | bytes 2097152

commit v8 on v7

--- a/solution.py
+++ b/solution.py
@@ -117,7 +117,7 @@
             when(cond, go)
             for name in names:
                 made, also = moves[name]
-                when(also, made[w].start)
+                when(cond if also is None else cond & also, made[w].start)
 
     def begin(which):
         for w in which:
@@ -263,12 +263,15 @@
     def pick(if_right, if_left):
         return col * if_right + (1 - col) * if_left
 
-    near = core * (8 + pos_m) + (1 - core) * pos_m
+    def sel(if_one, if_zero):
+        return core * if_one + (1 - core) * if_zero
+
+    core0, core1 = core == 0, core == 1
     pairs = (
-        (pick(8 + pos_x, 4 + pos), pick(8 + pos_d, 4 + pos_m), right | has1),
-        (pick(4 + pos, 4 + pos_x), pick(4 + pos_m, pos), has1),
-        (pick(4 + pos_x, 4 + pos_d), pick(4 + pos_d, near), has1 | (leftc & (core == 1))),
-        (pick(pos, pos_x), pick(near, pos_d), has2 | (right & (core == 1))),
+        (pick(8 + pos_x, 4 + pos), sel(8 + pos_m, pick(8 + pos_d, 4 + pos_m)), right | has1 | core1),
+        (pick(4 + pos, 4 + pos_x), pick(4 + pos_m, sel(4 + pos_m, pos)), has1),
+        (pick(4 + pos_x, 4 + pos_d), pick(4 + pos_d, sel(pos, pos_m)), has1),
+        (pick(pos, pos_x), pick(sel(8 + pos_d, pos_m), pos_d), has2 | (right & core1)),
     )
 
     def local(t):
@@ -302,8 +305,9 @@
         landed(8 + pos_x, right, "D0x", which=which)
 
     def first_over(which):
-        landed(4 + pos_m, has1, which=which)
-        landed(8 + pos_d, right, which=which)
+        landed(4 + pos_m, has1 & leftc & core0, which=which)
+        landed(8 + pos_d, right & core0, which=which)
+        landed(8 + pos_m, core1, which=which)
 
     @pl.loop(1, 12)
     def _(s):
@@ -319,34 +323,37 @@
 
     @pl.loop(0, 4)
     def _(i):
-        @pl.when(i == 1)
+        @pl.when(i == 2)
         def _():
             first_in(HIGH)
-
-        @pl.when(i == 2)
-        def _():
             first_over(HIGH)
 
         @pl.when(i == 3)
         def _():
-            landed(pos, has2, "X2", "D2", which=LOW)
-            landed(4 + pos_x, has1, "D1x", which=LOW)
+            landed(pos, has2 & core0, "X2", "D2", which=LOW)
+            landed(4 + pos_x, has1 & core0, "D1x", which=LOW)
 
         @pl.when(pairs[0][2])
         def _():
             sweep(i % 2 * swath, pairs[0][0], pairs[0][1], i // 2)
 
     def event1():
-        landed(pos, has2, "X2", "D2", which=HIGH)
+        landed(pos, has2 & core1, "X2", "D2", which=LOW)
+        landed(4 + pos_x, has1 & core1, "D1x", which=LOW)
         landed(4 + pos_x, has1, "D1x", which=HIGH)
+        landed(pos, has2 & core0, "X2", "D2", which=HIGH)
+        landed(4 + pos_m, has1 & (right | core1))
 
     def event2():
-        landed(8 + pos_m, None)
+        landed(pos, has2 & core1, "X2", "D2", which=HIGH)
+        landed(8 + pos_m, core0)
+        landed(8 + pos_d, right & core1)
         landed(4 + pos_d, has1)
         landed(pos_m, has2)
-        landed(pos_x, has2 & leftc, "D2x", which=LOW)
+        landed(pos_x, has2 & leftc & core0, "D2x", which=LOW)
 
     def event3():
+        landed(pos_x, has2 & leftc & core1, "D2x", which=LOW)
         landed(pos_x, has2 & leftc, "D2x", which=HIGH)
         landed(pos_d, has2 & leftc)
 

time: 39.6 us -> 38 us (0.960)
  Pallas kernels: 38.5 us -> 36.7 us
    pallas_call x1, Pallas kernels: 38.5 us -> 36.7 us  [on_device(): pl.pallas_call(functools.partial(kernel, n, heads, tile), out_shape=pltpu...]
where the time goes in v8:
time: 38 us; the launch traced here: 37.7 us
  Pallas kernels  36.7 us (97%)
  local copies, waits for them, and re-layouts  0.97 us (3%)
    pallas_call x1, Pallas kernels, on_device(): pl.pallas_call(functools.partial(kernel, n, heads, tile), out_shape=pltpu...  36.7 us
    unnamed x1, local copies, waits for them, and re-layouts  0.97 us

profile of v8, /device:TPU:25, one launch (start us, length us, event | category | flops | bytes accessed | tf_op | source)
XLA Modules:
  0.0 37.7 jit_solution(15164278574281451412)
XLA Ops:
  0.0 36.7 %shard_map.46 = bf16[256,2048]{1,0:T(8,128)(2,1)S(1)} custom-call(s32[32]{0:T(128)} %lens_in.1, bf16[4096,128]{1,0:T(8,128)(2,1)} %bitcast.3, bf16[512,128]{1,0:T(8,128)(2,1)} %bitcast.4, bf16[512,128]{1,0:T(8,128)(2,1)} %bitcast.5), custom_call_target="tpu_custom_call" | custom-call | tf_op jit(solution)/shard_map/pallas_call | solution.py:432
  36.7 1.0 %copy.6 = bf16[256,2048]{1,0:T(8,128)(2,1)} copy(bf16[256,2048]{1,0:T(8,128)(2,1)S(1)} %shard_map.46) | data formatting | bytes 2097152

commit v9 on v8

--- a/solution.py
+++ b/solution.py
@@ -145,7 +145,6 @@
     tokens = tile // group
     steps = part // tokens
     span = part * group
-    swath = total_rows // 2
 
     def by_token(width, dim):
         return lax.broadcasted_iota(jnp.int32, (tokens, group, width), dim).reshape(tile, width)
@@ -256,9 +255,9 @@
     def unit(first, a, b, extent):
         work(first, a, b, [(r, parts[w][2]) for r in range(0, extent, tile) for w in (0, 2)])
 
-    def sweep(first, a, b, h):
+    def sweep(a, b, h):
         where = pl.ds(pl.multiple_of(h * half_keys, half_keys), half_keys)
-        work(first, a, b, [(r, where) for r in range(0, swath, tile)])
+        work(0, a, b, [(r, where) for r in range(0, total_rows, tile)])
 
     def pick(if_right, if_left):
         return col * if_right + (1 - col) * if_left
@@ -269,8 +268,8 @@
     core0, core1 = core == 0, core == 1
     pairs = (
         (pick(8 + pos_x, 4 + pos), sel(8 + pos_m, pick(8 + pos_d, 4 + pos_m)), right | has1 | core1),
-        (pick(4 + pos, 4 + pos_x), pick(4 + pos_m, sel(4 + pos_m, pos)), has1),
-        (pick(4 + pos_x, 4 + pos_d), pick(4 + pos_d, sel(pos, pos_m)), has1),
+        (pick(4 + pos, 4 + pos_x), pick(4 + pos_m, sel(4 + pos_m, 4 + pos_d)), has1),
+        (pick(4 + pos_x, sel(4 + pos_d, pos)), pick(4 + pos_d, sel(pos, pos_m)), has2 | (has1 & (right | core1))),
         (pick(pos, pos_x), pick(sel(8 + pos_d, pos_m), pos_d), has2 | (right & core1)),
     )
 
@@ -321,40 +320,36 @@
     first_in(LOW)
     first_over(LOW)
 
-    @pl.loop(0, 4)
-    def _(i):
-        @pl.when(i == 2)
+    @pl.loop(0, 2)
+    def _(h):
+        @pl.when(h == 1)
         def _():
             first_in(HIGH)
             first_over(HIGH)
 
-        @pl.when(i == 3)
-        def _():
-            landed(pos, has2 & core0, "X2", "D2", which=LOW)
-            landed(4 + pos_x, has1 & core0, "D1x", which=LOW)
-
         @pl.when(pairs[0][2])
         def _():
-            sweep(i % 2 * swath, pairs[0][0], pairs[0][1], i // 2)
+            sweep(pairs[0][0], pairs[0][1], h)
 
     def event1():
-        landed(pos, has2 & core1, "X2", "D2", which=LOW)
-        landed(4 + pos_x, has1 & core1, "D1x", which=LOW)
-        landed(4 + pos_x, has1, "D1x", which=HIGH)
-        landed(pos, has2 & core0, "X2", "D2", which=HIGH)
+        landed(4 + pos_x, has1 & leftc, "D1x")
+        landed(4 + pos_x, has1 & right, "D1x", which=LOW)
+        landed(pos, has2 & right, "X2", "D2", which=LOW)
+        landed(pos, has2 & right & core0, "X2", "D2", which=HIGH)
         landed(4 + pos_m, has1 & (right | core1))
+        landed(4 + pos_d, has1 & leftc & core0)
 
     def event2():
-        landed(pos, has2 & core1, "X2", "D2", which=HIGH)
+        landed(pos, has2 & leftc, "D2")
+        landed(pos, has2 & right & core1, "X2", "D2", which=HIGH)
+        landed(4 + pos_x, has1 & right, "D1x", which=HIGH)
         landed(8 + pos_m, core0)
         landed(8 + pos_d, right & core1)
-        landed(4 + pos_d, has1)
+        landed(4 + pos_d, has1 & (right | core1))
         landed(pos_m, has2)
-        landed(pos_x, has2 & leftc & core0, "D2x", which=LOW)
 
     def event3():
-        landed(pos_x, has2 & leftc & core1, "D2x", which=LOW)
-        landed(pos_x, has2 & leftc, "D2x", which=HIGH)
+        landed(pos_x, has2 & leftc, "D2x")
         landed(pos_d, has2 & leftc)
 
     others = list(range(1, heads))

time: 38 us -> 38.3 us (level)
  the two profiles are of different devices: /device:TPU:25 before, /device:TPU:16 now
where the time goes in v9:
time: 38.3 us; the launch traced here: 38.1 us
  Pallas kernels  37.1 us (97%)
  local copies, waits for them, and re-layouts  0.97 us (3%)
    pallas_call x1, Pallas kernels, on_device(): pl.pallas_call(functools.partial(kernel, n, heads, tile), out_shape=pltpu...  37.1 us
    unnamed x1, local copies, waits for them, and re-layouts  0.97 us

profile of v9, /device:TPU:16, one launch (start us, length us, event | category | flops | bytes accessed | tf_op | source)
XLA Modules:
  0.0 38.1 jit_solution(11087873312419404554)
XLA Ops:
  0.0 37.1 %shard_map.46 = bf16[256,2048]{1,0:T(8,128)(2,1)S(1)} custom-call(s32[32]{0:T(128)} %lens_in.1, bf16[4096,128]{1,0:T(8,128)(2,1)} %bitcast.3, bf16[512,128]{1,0:T(8,128)(2,1)} %bitcast.4, bf16[512,128]{1,0:T(8,128)(2,1)} %bitcast.5), custom_call_target="tpu_custom_call" | custom-call | tf_op jit(solution)/shard_map/pallas_call | solution.py:427
  37.2 1.0 %copy.6 = bf16[256,2048]{1,0:T(8,128)(2,1)} copy(bf16[256,2048]{1,0:T(8,128)(2,1)S(1)} %shard_map.46) | data formatting | bytes 2097152

commit v10 on v9

--- a/solution.py
+++ b/solution.py
@@ -336,21 +336,23 @@
         landed(4 + pos_x, has1 & right, "D1x", which=LOW)
         landed(pos, has2 & right, "X2", "D2", which=LOW)
         landed(pos, has2 & right & core0, "X2", "D2", which=HIGH)
+        landed(4 + pos_x, has1 & right & core0, "D1x", which=HIGH)
         landed(4 + pos_m, has1 & (right | core1))
         landed(4 + pos_d, has1 & leftc & core0)
 
     def event2():
         landed(pos, has2 & leftc, "D2")
         landed(pos, has2 & right & core1, "X2", "D2", which=HIGH)
-        landed(4 + pos_x, has1 & right, "D1x", which=HIGH)
-        landed(8 + pos_m, core0)
-        landed(8 + pos_d, right & core1)
+        landed(4 + pos_x, has1 & right & core1, "D1x", which=HIGH)
         landed(4 + pos_d, has1 & (right | core1))
-        landed(pos_m, has2)
+        landed(pos_m, has2 & leftc & core0)
 
     def event3():
         landed(pos_x, has2 & leftc, "D2x")
         landed(pos_d, has2 & leftc)
+        landed(8 + pos_m, core0)
+        landed(8 + pos_d, right & core1)
+        landed(pos_m, has2 & (right | core1))
 
     others = list(range(1, heads))
     order = [(p, d) for p in ORDER for d in (others if p < 4 else [heads])]

time: 38.3 us -> 37.5 us (0.979)
  the two profiles are of different devices: /device:TPU:16 before, /device:TPU:25 now
where the time goes in v10:
time: 37.5 us; the launch traced here: 37.2 us
  Pallas kernels  36.2 us (97%)
  local copies, waits for them, and re-layouts  0.97 us (3%)
    pallas_call x1, Pallas kernels, on_device(): pl.pallas_call(functools.partial(kernel, n, heads, tile), out_shape=pltpu...  36.2 us
    unnamed x1, local copies, waits for them, and re-layouts  0.97 us

profile of v10, /device:TPU:25, one launch (start us, length us, event | category | flops | bytes accessed | tf_op | source)
XLA Modules:
  0.0 37.2 jit_solution(9924972281334539459)
XLA Ops:
  0.0 36.2 %shard_map.46 = bf16[256,2048]{1,0:T(8,128)(2,1)S(1)} custom-call(s32[32]{0:T(128)} %lens_in.1, bf16[4096,128]{1,0:T(8,128)(2,1)} %bitcast.3, bf16[512,128]{1,0:T(8,128)(2,1)} %bitcast.4, bf16[512,128]{1,0:T(8,128)(2,1)} %bitcast.5), custom_call_target="tpu_custom_call" | custom-call | tf_op jit(solution)/shard_map/pallas_call | solution.py:429
  36.2 1.0 %copy.6 = bf16[256,2048]{1,0:T(8,128)(2,1)} copy(bf16[256,2048]{1,0:T(8,128)(2,1)S(1)} %shard_map.46) | data formatting | bytes 2097152

commit v11 on v10

--- a/solution.py
+++ b/solution.py
@@ -326,13 +326,14 @@
         def _():
             first_in(HIGH)
             first_over(HIGH)
+            landed(4 + pos_x, has1 & leftc, "D1x", which=LOW)
 
         @pl.when(pairs[0][2])
         def _():
             sweep(pairs[0][0], pairs[0][1], h)
 
     def event1():
-        landed(4 + pos_x, has1 & leftc, "D1x")
+        landed(4 + pos_x, has1 & leftc, "D1x", which=HIGH)
         landed(4 + pos_x, has1 & right, "D1x", which=LOW)
         landed(pos, has2 & right, "X2", "D2", which=LOW)
         landed(pos, has2 & right & core0, "X2", "D2", which=HIGH)
@@ -346,9 +347,10 @@
         landed(4 + pos_x, has1 & right & core1, "D1x", which=HIGH)
         landed(4 + pos_d, has1 & (right | core1))
         landed(pos_m, has2 & leftc & core0)
+        landed(pos_x, has2 & leftc, "D2x", which=LOW)
 
     def event3():
-        landed(pos_x, has2 & leftc, "D2x")
+        landed(pos_x, has2 & leftc, "D2x", which=HIGH)
         landed(pos_d, has2 & leftc)
         landed(8 + pos_m, core0)
         landed(8 + pos_d, right & core1)

time: 37.5 us -> 37.5 us (level)
  no operation moved by 1% of the time
where the time goes in v11:
time: 37.5 us; the launch traced here: 37.2 us
  Pallas kernels  36.2 us (97%)
  local copies, waits for them, and re-layouts  0.97 us (3%)
    pallas_call x1, Pallas kernels, on_device(): pl.pallas_call(functools.partial(kernel, n, heads, tile), out_shape=pltpu...  36.2 us
    unnamed x1, local copies, waits for them, and re-layouts  0.97 us

profile of v11, /device:TPU:25, one launch (start us, length us, event | category | flops | bytes accessed | tf_op | source)
XLA Modules:
  0.0 37.2 jit_solution(6133431241856854571)
XLA Ops:
  0.0 36.2 %shard_map.46 = bf16[256,2048]{1,0:T(8,128)(2,1)S(1)} custom-call(s32[32]{0:T(128)} %lens_in.1, bf16[4096,128]{1,0:T(8,128)(2,1)} %bitcast.3, bf16[512,128]{1,0:T(8,128)(2,1)} %bitcast.4, bf16[512,128]{1,0:T(8,128)(2,1)} %bitcast.5), custom_call_target="tpu_custom_call" | custom-call | tf_op jit(solution)/shard_map/pallas_call | solution.py:431
  36.2 1.0 %copy.6 = bf16[256,2048]{1,0:T(8,128)(2,1)} copy(bf16[256,2048]{1,0:T(8,128)(2,1)S(1)} %shard_map.46) | data formatting | bytes 2097152

commit v12 on v11

--- a/solution.py
+++ b/solution.py
@@ -78,7 +78,7 @@
         ) for w, (own, buf, where) in enumerate(parts)]
 
     moves = {
-        "D0": (copies(0, None, 8 + pos, mate), None),
+        "D0": (copies(0, None, 8 + pos, mate), core == 0),
         "X0": (copies(1, None, 8 + pos, across), leftc),
         "Z0": (copies(2, None, 4 + pos, me + 4), feeds),
         "D0x": (copies(3, 8 + pos_x, 8 + pos_x, mate), right),
@@ -86,7 +86,7 @@
         "X1": (copies(5, 4 + pos, 4 + pos, across), has1),
         "Z1": (copies(6, 4 + pos, pos, me + 4), has1 & feeds),
         "D1x": (copies(7, 4 + pos_x, 4 + pos_x, mate), has1),
-        "D2": (copies(8, pos, pos, mate), has2),
+        "D2": (copies(8, pos, pos, mate), has2 & (core == 1)),
         "X2": (copies(9, pos, pos, across), has2 & right),
         "D2x": (copies(10, pos_x, pos_x, mate), has2 & leftc),
     }
@@ -326,14 +326,13 @@
         def _():
             first_in(HIGH)
             first_over(HIGH)
-            landed(4 + pos_x, has1 & leftc, "D1x", which=LOW)
 
         @pl.when(pairs[0][2])
         def _():
             sweep(pairs[0][0], pairs[0][1], h)
 
     def event1():
-        landed(4 + pos_x, has1 & leftc, "D1x", which=HIGH)
+        landed(4 + pos_x, has1 & leftc, "D1x")
         landed(4 + pos_x, has1 & right, "D1x", which=LOW)
         landed(pos, has2 & right, "X2", "D2", which=LOW)
         landed(pos, has2 & right & core0, "X2", "D2", which=HIGH)
@@ -352,9 +351,8 @@
     def event3():
         landed(pos_x, has2 & leftc, "D2x", which=HIGH)
         landed(pos_d, has2 & leftc)
-        landed(8 + pos_m, core0)
         landed(8 + pos_d, right & core1)
-        landed(pos_m, has2 & (right | core1))
+        landed(pos_m, has2 & right & core0)
 
     others = list(range(1, heads))
     order = [(p, d) for p in ORDER for d in (others if p < 4 else [heads])]

time: 37.5 us -> 37.5 us (level)
  no operation moved by 1% of the time
where the time goes in v12:
time: 37.5 us; the launch traced here: 37.1 us
  Pallas kernels  36.2 us (97%)
  local copies, waits for them, and re-layouts  0.97 us (3%)
    pallas_call x1, Pallas kernels, on_device(): pl.pallas_call(functools.partial(kernel, n, heads, tile), out_shape=pltpu...  36.2 us
    unnamed x1, local copies, waits for them, and re-layouts  0.97 us

profile of v12, /device:TPU:25, one launch (start us, length us, event | category | flops | bytes accessed | tf_op | source)
XLA Modules:
  0.0 37.1 jit_solution(11092082779648414348)
XLA Ops:
  0.0 36.2 %shard_map.46 = bf16[256,2048]{1,0:T(8,128)(2,1)S(1)} custom-call(s32[32]{0:T(128)} %lens_in.1, bf16[4096,128]{1,0:T(8,128)(2,1)} %bitcast.3, bf16[512,128]{1,0:T(8,128)(2,1)} %bitcast.4, bf16[512,128]{1,0:T(8,128)(2,1)} %bitcast.5), custom_call_target="tpu_custom_call" | custom-call | tf_op jit(solution)/shard_map/pallas_call | solution.py:429
  36.2 1.0 %copy.6 = bf16[256,2048]{1,0:T(8,128)(2,1)} copy(bf16[256,2048]{1,0:T(8,128)(2,1)S(1)} %shard_map.46) | data formatting | bytes 2097152

commit v13 on v12

--- a/solution.py
+++ b/solution.py
@@ -13,6 +13,7 @@
 MOST = 512
 BAND = 128
 ORDER = (1, 2, 3, 5, 6, 7)
+FILLED = (1, 2, 5, 3, 6, 7)
 LOW, HIGH = (0, 1), (2, 3)
 ALL = LOW + HIGH
 
@@ -350,25 +351,32 @@
 
     def event3():
         landed(pos_x, has2 & leftc, "D2x", which=HIGH)
+
+    def event4():
         landed(pos_d, has2 & leftc)
         landed(8 + pos_d, right & core1)
         landed(pos_m, has2 & right & core0)
 
     others = list(range(1, heads))
-    order = [(p, d) for p in ORDER for d in (others if p < 4 else [heads])]
-    order = [(p % 4, d) for p, d in order]
-    kinds = [p if d < heads else p + 4 for p, d in order]
-    events = ((1, event1), (2, event2), (3, event3))
+    plans = [[(p % 4, d) for p in order for d in (others if p < 4 else [heads])] for order in (ORDER, FILLED)]
+    kinds = [[p if d < heads else p + 4 for p, d in plan] for plan in plans]
+    filled = (leftc & core1).astype(jnp.int32)
+    spots = [[kind.index(p) for kind in kinds] for p in (1, 2, 3)]
+    events = (
+        (spots[0], event1), (spots[1], event2), ([min(spots[2])] * 2, event3), (spots[2], event4))
+
+    def either(pair):
+        return filled * pair[1] + (1 - filled) * pair[0]
 
     def choose(index, values):
         return sum((index == i) * jnp.asarray(x, jnp.int32) for i, x in enumerate(values))
 
-    @pl.loop(0, len(order))
+    @pl.loop(0, len(plans[0]))
     def _(u):
-        for kind, event in events:
-            pl.when(u == kinds.index(kind))(event)
-        p = choose(u, [x for x, _ in order])
-        d = choose(u, [x for _, x in order])
+        for places, event in events:
+            pl.when(u == either(places))(event)
+        p = either([choose(u, [x for x, _ in plan]) for plan in plans])
+        d = either([choose(u, [x for _, x in plan]) for plan in plans])
         first = (mine + d) % heads * span
 
         valid = choose(p, [x[2] for x in pairs]) == 1

time: 37.5 us -> 37.5 us (level)
  no operation moved by 1% of the time
where the time goes in v13:
time: 37.5 us; the launch traced here: 37.1 us
  Pallas kernels  36.2 us (97%)
  local copies, waits for them, and re-layouts  0.97 us (3%)
    pallas_call x1, Pallas kernels, on_device(): pl.pallas_call(functools.partial(kernel, n, heads, tile), out_shape=pltpu...  36.2 us
    unnamed x1, local copies, waits for them, and re-layouts  0.97 us

profile of v13, /device:TPU:25, one launch (start us, length us, event | category | flops | bytes accessed | tf_op | source)
XLA Modules:
  0.0 37.1 jit_solution(14848556041555964730)
XLA Ops:
  0.0 36.2 %shard_map.46 = bf16[256,2048]{1,0:T(8,128)(2,1)S(1)} custom-call(s32[32]{0:T(128)} %lens_in.1, bf16[4096,128]{1,0:T(8,128)(2,1)} %bitcast.3, bf16[512,128]{1,0:T(8,128)(2,1)} %bitcast.4, bf16[512,128]{1,0:T(8,128)(2,1)} %bitcast.5), custom_call_target="tpu_custom_call" | custom-call | tf_op jit(solution)/shard_map/pallas_call | solution.py:437
  36.2 1.0 %copy.6 = bf16[256,2048]{1,0:T(8,128)(2,1)} copy(bf16[256,2048]{1,0:T(8,128)(2,1)S(1)} %shard_map.46) | data formatting | bytes 2097152

commit v14 on v13

--- a/solution.py
+++ b/solution.py
@@ -301,7 +301,7 @@
     begin(HIGH)
 
     def first_in(which):
-        landed(4 + pos, has1, "Z1", "X1", "D1", which=which)
+        landed(4 + pos, has1, "X1", "Z1", "D1", which=which)
         landed(8 + pos_x, right, "D0x", which=which)
 
     def first_over(which):
@@ -327,13 +327,15 @@
         def _():
             first_in(HIGH)
             first_over(HIGH)
+            landed(4 + pos_x, has1 & leftc & core1, "D1x", which=LOW)
 
         @pl.when(pairs[0][2])
         def _():
             sweep(pairs[0][0], pairs[0][1], h)
 
     def event1():
-        landed(4 + pos_x, has1 & leftc, "D1x")
+        landed(4 + pos_x, has1 & leftc & core0, "D1x", which=LOW)
+        landed(4 + pos_x, has1 & leftc, "D1x", which=HIGH)
         landed(4 + pos_x, has1 & right, "D1x", which=LOW)
         landed(pos, has2 & right, "X2", "D2", which=LOW)
         landed(pos, has2 & right & core0, "X2", "D2", which=HIGH)

time: 37.5 us -> 37.5 us (level)
  no operation moved by 1% of the time
where the time goes in v14:
time: 37.5 us; the launch traced here: 37.1 us
  Pallas kernels  36.1 us (96%)
  local copies, waits for them, and re-layouts  0.97 us (3%)
    pallas_call x1, Pallas kernels, on_device(): pl.pallas_call(functools.partial(kernel, n, heads, tile), out_shape=pltpu...  36.1 us
    unnamed x1, local copies, waits for them, and re-layouts  0.97 us

profile of v14, /device:TPU:25, one launch (start us, length us, event | category | flops | bytes accessed | tf_op | source)
XLA Modules:
  0.0 37.1 jit_solution(16342150239411929250)
XLA Ops:
  0.0 36.1 %shard_map.46 = bf16[256,2048]{1,0:T(8,128)(2,1)S(1)} custom-call(s32[32]{0:T(128)} %lens_in.1, bf16[4096,128]{1,0:T(8,128)(2,1)} %bitcast.3, bf16[512,128]{1,0:T(8,128)(2,1)} %bitcast.4, bf16[512,128]{1,0:T(8,128)(2,1)} %bitcast.5), custom_call_target="tpu_custom_call" | custom-call | tf_op jit(solution)/shard_map/pallas_call | solution.py:439
  36.1 1.0 %copy.6 = bf16[256,2048]{1,0:T(8,128)(2,1)} copy(bf16[256,2048]{1,0:T(8,128)(2,1)S(1)} %shard_map.46) | data formatting | bytes 2097152
